TPU v7x, 32 devices: a whole 2x2x4 slice. The times are simulated.
32 devices in a mesh: px: 8 (over z, y), py: 4 (over x, core).
Axes of the slice: x: 2, y: 2, z: 4, core: 2. Of those that a mesh axis runs over, the one named last changes fastest.
Arguments:
- initial_field: float32 [1, 2048, 2048], P(None, ('px', 'py')), may hold values from -6 to 6
- target_field: float32 [1, 2048, 2048], P(None, ('px', 'py')), may hold values from -6 to 6
- forcing: float32 [2, 2048, 2048], P(None, ('px', 'py')), may hold values from -6 to 6
Outputs:
- next_field: float32 [1, 2048, 2048], P(None, ('px', 'py'))
- objective: float32 [], replicated
- field_grad: float32 [1, 2048, 2048], P(None, ('px', 'py'))
- forcing_grad: float32 [2, 2048, 2048], P(None, ('px', 'py'))
All inputs are finite; a program needn't handle non-finite values.
Results may differ from a plain program's by a relative error of at most 0.00014.
Values sent between devices are 32-bit elements; how exact they have to be, the bound alone decides.
A program may use at most 128 MiB of HBM per device.

v0:
```python
import math

import jax
import jax.numpy as jnp
from jax import lax
from jax.sharding import PartitionSpec as P

time_step = 0.25
highest = lax.Precision.HIGHEST


def factor_pair(length):
    first_len = int(math.isqrt(length))
    while length % first_len:
        first_len -= 1
    return (first_len, length // first_len)


def phases(row_count, col_count, period, sign_value, factor):
    product = (
        jnp.arange(row_count, dtype=jnp.int32)[:, None]
        * jnp.arange(col_count, dtype=jnp.int32)[None, :]
        % period
    )
    angles = product.astype(jnp.float32) * (2.0 * math.pi / period)
    return (factor * jnp.cos(angles), sign_value * factor * jnp.sin(angles))


def complex_einsum(formula, left_real, left_imag, table_pair):
    real_term = jnp.einsum(formula, left_real, table_pair[0], precision=highest)
    imag_term = jnp.einsum(formula, left_real, table_pair[1], precision=highest)
    if left_imag is None:
        return (real_term, imag_term)
    real_term = real_term - jnp.einsum(formula, left_imag, table_pair[1], precision=highest)
    imag_term = imag_term + jnp.einsum(formula, left_imag, table_pair[0], precision=highest)
    return (real_term, imag_term)


def transform(real_part, imag_part, sign_value, leading, real_only):
    if leading:
        members, length, span_rows = real_part.shape
        first_len, second_len = factor_pair(length)
        new_shape = (members, first_len, second_len, span_rows)
        formula = "mabr,ak->mrkb"
    else:
        members, span_rows, length = real_part.shape
        first_len, second_len = factor_pair(length)
        new_shape = (members, span_rows, first_len, second_len)
        formula = "mrab,ak->mrkb"
    shaped_real = real_part.reshape(new_shape)
    shaped_imag = None if imag_part is None else imag_part.reshape(new_shape)
    sectioned_out = complex_einsum(
        formula, shaped_real, shaped_imag, phases(first_len, first_len, first_len, sign_value, 1.0)
    )
    twiddle = phases(first_len, second_len, length, sign_value, 1.0 / math.sqrt(length))
    turned_real = sectioned_out[0] * twiddle[0] - sectioned_out[1] * twiddle[1]
    turned_imag = sectioned_out[0] * twiddle[1] + sectioned_out[1] * twiddle[0]
    last_table = phases(second_len, second_len, second_len, sign_value, 1.0)
    final_formula = "mrkb,bq->mrqk"
    if real_only:
        out_real = jnp.einsum(final_formula, turned_real, last_table[0], precision=highest)
        out_real = out_real - jnp.einsum(
            final_formula, turned_imag, last_table[1], precision=highest
        )
        return (out_real.reshape(members, span_rows, length), None)
    out_real, out_imag = complex_einsum(final_formula, turned_real, turned_imag, last_table)
    return (
        out_real.reshape(members, span_rows, length),
        out_imag.reshape(members, span_rows, length),
    )


def regroup(real_part, imag_part):
    moved_real, moved_imag = (
        lax.all_to_all(real_part, ("px", "py"), split_axis=2, concat_axis=1, tiled=True),
        lax.all_to_all(imag_part, ("px", "py"), split_axis=2, concat_axis=1, tiled=True),
    )
    return (moved_real, moved_imag)


def spectral(real_part, imag_part):
    first_pass = transform(real_part, imag_part, -1.0, False, False)
    moved = regroup(first_pass[0], first_pass[1])
    return transform(moved[0], moved[1], -1.0, True, False)


def physical(real_part, imag_part, real_only):
    first_pass = transform(real_part, imag_part, 1.0, False, False)
    moved = regroup(first_pass[0], first_pass[1])
    return transform(moved[0], moved[1], 1.0, True, real_only)


def waves_of(position, count):
    signed = jnp.where(position < count // 2, position, position - count)
    waves = 4.0 * signed.astype(jnp.float32) / count
    derive = jnp.where(position == count // 2, jnp.float32(0.0), waves)
    return (waves, derive)


def per_device(initial_field, target_field, forcing):
    members = initial_field.shape[0]
    full_second = initial_field.shape[2]
    spec_rows = forcing.shape[1]
    full_first = forcing.shape[2]
    device = lax.axis_index(("px", "py"))
    position_first = jnp.arange(full_first, dtype=jnp.int32)
    position_second = device * spec_rows + jnp.arange(spec_rows, dtype=jnp.int32)
    wave_first, deriv_first = waves_of(position_first, full_first)
    wave_second, deriv_second = waves_of(position_second, full_second)
    wave_first = wave_first[None, :]
    deriv_first = deriv_first[None, :]
    wave_second = wave_second[:, None]
    deriv_second = deriv_second[:, None]
    wave_square = wave_first * wave_first + wave_second * wave_second
    denominator = 1.0 + time_step * (wave_square * wave_square - wave_square)
    state_real, state_imag = spectral(initial_field, None)
    slope_real = -deriv_first * state_imag - deriv_second * state_real
    slope_imag = deriv_first * state_real - deriv_second * state_imag
    grad_first, grad_second = physical(slope_real, slope_imag, False)
    nonlinear = -0.5 * (grad_first * grad_first + grad_second * grad_second)
    nonlinear_real, nonlinear_imag = spectral(nonlinear, None)
    next_real = (state_real + time_step * (nonlinear_real + forcing[0])) / denominator
    next_imag = (state_imag + time_step * (nonlinear_imag + forcing[1])) / denominator
    next_field, unused_part = physical(next_real, next_imag, True)
    residual = next_field - target_field
    total = lax.psum(0.5 * jnp.sum(residual * residual), ("px", "py"))
    objective = total / (members * full_first * full_second)
    misfit_real, misfit_imag = spectral(residual, None)
    coef_real = misfit_real / denominator
    coef_imag = misfit_imag / denominator
    forcing_grad = time_step * jnp.stack([jnp.sum(coef_real, axis=0), jnp.sum(coef_imag, axis=0)])
    multiplier, unused_other = physical(time_step * coef_real, time_step * coef_imag, True)
    joint_real, joint_imag = spectral(multiplier * grad_first, multiplier * grad_second)
    total_real = coef_real - deriv_first * joint_imag + deriv_second * joint_real
    total_imag = coef_imag + deriv_first * joint_real + deriv_second * joint_imag
    field_grad, unused_last = physical(total_real, total_imag, True)
    return (next_field, objective, field_grad, forcing_grad)


def solution(mesh):
    return jax.shard_map(
        per_device,
        mesh=mesh,
        in_specs=(
            P(None, ("px", "py"), None),
            P(None, ("px", "py"), None),
            P(None, ("px", "py"), None),
        ),
        out_specs=(
            P(None, ("px", "py"), None),
            P(),
            P(None, ("px", "py"), None),
            P(None, ("px", "py"), None),
        ),
        check_vma=False,
    )
```

profile of v0, /device:TPU:0, one launch (start us, length us, event | category | flops | bytes accessed | tf_op | source)
XLA Modules:
  0.0 883.1 jit_solution(13582286991271843873)
XLA Ops:
  13.7 10.5 %reduce = f32[2048,64]{1,0:T(8,128)S(1)} reduce(f32[2048,1,64]{2,1,0:T(1,128)} %bitcast.931, f32[]{:T(128)} %broadcast.1623), dimensions={1}, to_apply=%bitcast.761.reduce_sub_computation | reduce | bytes 1048580
  25.6 7.3 all-to-all-start
  40.6 9.3 %reduce.2 = f32[2048,64]{1,0:T(8,128)S(1)} reduce(f32[2048,1,64]{2,1,0:T(1,128)S(1)} %bitcast.932, f32[]{:T(128)} %broadcast.1623), dimensions={1}, to_apply=%bitcast.763.reduce_sub_computation | reduce | bytes 1048580
  65.1 8.1 all-to-all-done.1
  123.8 11.5 %reduce.4 = f32[2048,64]{1,0:T(8,128)} reduce(f32[2048,1,64]{2,1,0:T(1,128)} %bitcast.933, f32[]{:T(128)} %broadcast.1623), dimensions={1}, to_apply=%bitcast.765.reduce_sub_computation | reduce | bytes 1048580
  151.2 10.3 %reduce.6 = f32[2048,64]{1,0:T(8,128)S(1)} reduce(f32[2048,1,64]{2,1,0:T(1,128)} %bitcast.934, f32[]{:T(128)} %broadcast.1623), dimensions={1}, to_apply=%bitcast.767.reduce_sub_computation | reduce | bytes 1048580
  162.9 6.3 all-to-all-start.3
  234.5 11.3 %reduce.8 = f32[2048,64]{1,0:T(8,128)} reduce(f32[2048,1,64]{2,1,0:T(1,128)} %bitcast.935, f32[]{:T(128)} %broadcast.1623), dimensions={1}, to_apply=%bitcast.769.reduce_sub_computation | reduce | bytes 1048580
  262.0 10.3 %reduce.10 = f32[2048,64]{1,0:T(8,128)S(1)} reduce(f32[2048,1,64]{2,1,0:T(1,128)} %bitcast.936, f32[]{:T(128)} %broadcast.1623), dimensions={1}, to_apply=%bitcast.771.reduce_sub_computation | reduce | bytes 1048580
  349.9 10.3 %reduce.12 = f32[2048,64]{1,0:T(8,128)S(1)} reduce(f32[2048,1,64]{2,1,0:T(1,128)} %bitcast.937, f32[]{:T(128)} %broadcast.1623), dimensions={1}, to_apply=%bitcast.773.reduce_sub_computation | reduce | bytes 1048580
  375.6 9.3 %reduce.14 = f32[2048,64]{1,0:T(8,128)S(1)} reduce(f32[2048,1,64]{2,1,0:T(1,128)S(1)} %bitcast.938, f32[]{:T(128)} %broadcast.1623), dimensions={1}, to_apply=%bitcast.775.reduce_sub_computation | reduce | bytes 1048580
  401.2 6.8 all-to-all-done.7
  436.4 10.3 %reduce.16 = f32[2048,64]{1,0:T(8,128)S(1)} reduce(f32[2048,1,64]{2,1,0:T(1,128)} %bitcast.939, f32[]{:T(128)} %broadcast.1623), dimensions={1}, to_apply=%bitcast.777.reduce_sub_computation | reduce | bytes 1048580
  458.7 9.3 %reduce.18 = f32[2048,64]{1,0:T(8,128)S(1)} reduce(f32[2048,1,64]{2,1,0:T(1,128)S(1)} %bitcast.940, f32[]{:T(128)} %broadcast.1623), dimensions={1}, to_apply=%bitcast.779.reduce_sub_computation | reduce | bytes 1048580
  483.0 8.3 all-to-all-done.9
  542.0 11.3 %reduce.20 = f32[2048,64]{1,0:T(8,128)} reduce(f32[2048,1,64]{2,1,0:T(1,128)} %bitcast.941, f32[]{:T(128)} %broadcast.1623), dimensions={1}, to_apply=%bitcast.781.reduce_sub_computation | reduce | bytes 1048580
  569.3 10.3 %reduce.22 = f32[2048,64]{1,0:T(8,128)S(1)} reduce(f32[2048,1,64]{2,1,0:T(1,128)} %bitcast.942, f32[]{:T(128)} %broadcast.1623), dimensions={1}, to_apply=%bitcast.783.reduce_sub_computation | reduce | bytes 1048580
  581.0 6.3 all-to-all-start.11
  645.4 11.3 %reduce.24 = f32[2048,64]{1,0:T(8,128)} reduce(f32[2048,1,64]{2,1,0:T(1,128)} %bitcast.943, f32[]{:T(128)} %broadcast.1623), dimensions={1}, to_apply=%bitcast.785.reduce_sub_computation | reduce | bytes 1048580
  672.8 10.3 %reduce.26 = f32[2048,64]{1,0:T(8,128)S(1)} reduce(f32[2048,1,64]{2,1,0:T(1,128)} %bitcast.944, f32[]{:T(128)} %broadcast.1623), dimensions={1}, to_apply=%bitcast.787.reduce_sub_computation | reduce | bytes 1048580
  684.5 6.5 all-to-all-start.13
  765.7 11.5 %reduce.28 = f32[2048,64]{1,0:T(8,128)} reduce(f32[2048,1,64]{2,1,0:T(1,128)} %bitcast.945, f32[]{:T(128)} %broadcast.1623), dimensions={1}, to_apply=%bitcast.789.reduce_sub_computation | reduce | bytes 1048580
  783.8 40.5 %psum.7 = f32[]{:T(128)} all-reduce(f32[]{:T(128)S(6)} %mul_shard_map.3), channel_id=1, replica_groups=mesh['px'=8,'py'=4] {'px','py'}, use_global_device_ids=true, to_apply=%region_1.2 | all-reduce | flops 1 | bytes 8 | tf_op jit(solution)/shard_map/psum | solution.py:126
  837.1 10.3 %reduce.30 = f32[2048,64]{1,0:T(8,128)S(1)} reduce(f32[2048,1,64]{2,1,0:T(1,128)} %bitcast.946, f32[]{:T(128)} %broadcast.1623), dimensions={1}, to_apply=%bitcast.791.reduce_sub_computation | reduce | bytes 1048580
  (358 shorter events, 620.8 us)
Async XLA Ops:
  25.6 25.7 %all-to-all-start = ((f32[32,1,4096]{2,1,0:T(1,128)}), f32[32,1,4096]{2,1,0:T(1,128)S(1)}, u32[]{:S(2)}, u32[]{:S(2)}) async-start(f32[32,1,4096]{2,1,0:T(1,128)} %reshape.1269), calls=%async_computation | async-start | bytes 1048576 | tf_op jit(solution)/shard_map/all_to_all | solution.py:75
  51.3 21.9 %all-to-all-start.1 = ((f32[32,1,4096]{2,1,0:T(1,128)}), f32[32,1,4096]{2,1,0:T(1,128)S(1)}, u32[]{:S(2)}, u32[]{:S(2)}) async-start(f32[32,1,4096]{2,1,0:T(1,128)} %reshape.1271), calls=%async_computation.1 | async-start | bytes 1048576 | tf_op jit(solution)/shard_map/all_to_all | solution.py:76
  115.2 7.1 copy-start.10
  138.0 24.9 %all-to-all-start.2 = ((f32[32,1,4096]{2,1,0:T(1,128)}), f32[32,1,4096]{2,1,0:T(1,128)}, u32[]{:S(2)}, u32[]{:S(2)}) async-start(f32[32,1,4096]{2,1,0:T(1,128)} %reshape.1273), calls=%async_computation.2 | async-start | bytes 1048576 | tf_op jit(solution)/shard_map/all_to_all | solution.py:75
  162.9 21.9 %all-to-all-start.3 = ((f32[32,1,4096]{2,1,0:T(1,128)}), f32[32,1,4096]{2,1,0:T(1,128)}, u32[]{:S(2)}, u32[]{:S(2)}) async-start(f32[32,1,4096]{2,1,0:T(1,128)} %reshape.1275), calls=%async_computation.3 | async-start | bytes 1048576 | tf_op jit(solution)/shard_map/all_to_all | solution.py:76
  225.7 7.2 copy-start.13
  248.5 25.3 %all-to-all-start.4 = ((f32[32,1,4096]{2,1,0:T(1,128)}), f32[32,1,4096]{2,1,0:T(1,128)}, u32[]{:S(2)}, u32[]{:S(2)}) async-start(f32[32,1,4096]{2,1,0:T(1,128)} %reshape.1277), calls=%async_computation.4 | async-start | bytes 1048576 | tf_op jit(solution)/shard_map/all_to_all | solution.py:75
  273.8 21.8 %all-to-all-start.5 = ((f32[32,1,4096]{2,1,0:T(1,128)}), f32[32,1,4096]{2,1,0:T(1,128)}, u32[]{:S(2)}, u32[]{:S(2)}) async-start(f32[32,1,4096]{2,1,0:T(1,128)} %reshape.1279), calls=%async_computation.5 | async-start | bytes 1048576 | tf_op jit(solution)/shard_map/all_to_all | solution.py:76
  320.5 5.1 copy-start.20
  361.6 24.7 %all-to-all-start.6 = ((f32[32,1,4096]{2,1,0:T(1,128)}), f32[32,1,4096]{2,1,0:T(1,128)}, u32[]{:S(2)}, u32[]{:S(2)}) async-start(f32[32,1,4096]{2,1,0:T(1,128)} %reshape.1281), calls=%async_computation.6 | async-start | bytes 1048576 | tf_op jit(solution)/shard_map/all_to_all | solution.py:75
  384.8 7.7 copy-start.37
  386.3 21.7 %all-to-all-start.7 = ((f32[32,1,4096]{2,1,0:T(1,128)}), f32[32,1,4096]{2,1,0:T(1,128)}, u32[]{:S(2)}, u32[]{:S(2)}) async-start(f32[32,1,4096]{2,1,0:T(1,128)} %reshape.1283), calls=%async_computation.7 | async-start | bytes 1048576 | tf_op jit(solution)/shard_map/all_to_all | solution.py:76
  448.1 21.3 %all-to-all-start.8 = ((f32[32,1,4096]{2,1,0:T(1,128)}), f32[32,1,4096]{2,1,0:T(1,128)S(1)}, u32[]{:S(2)}, u32[]{:S(2)}) async-start(f32[32,1,4096]{2,1,0:T(1,128)} %reshape.1285), calls=%async_computation.8 | async-start | bytes 1048576 | tf_op jit(solution)/shard_map/all_to_all | solution.py:75
  469.4 21.9 %all-to-all-start.9 = ((f32[32,1,4096]{2,1,0:T(1,128)}), f32[32,1,4096]{2,1,0:T(1,128)S(1)}, u32[]{:S(2)}, u32[]{:S(2)}) async-start(f32[32,1,4096]{2,1,0:T(1,128)} %reshape.1287), calls=%async_computation.9 | async-start | bytes 1048576 | tf_op jit(solution)/shard_map/all_to_all | solution.py:76
  533.3 7.0 copy-start.11
  555.9 25.1 %all-to-all-start.10 = ((f32[32,1,4096]{2,1,0:T(1,128)}), f32[32,1,4096]{2,1,0:T(1,128)}, u32[]{:S(2)}, u32[]{:S(2)}) async-start(f32[32,1,4096]{2,1,0:T(1,128)} %reshape.1289), calls=%async_computation.10 | async-start | bytes 1048576 | tf_op jit(solution)/shard_map/all_to_all | solution.py:75
  581.0 21.7 %all-to-all-start.11 = ((f32[32,1,4096]{2,1,0:T(1,128)}), f32[32,1,4096]{2,1,0:T(1,128)}, u32[]{:S(2)}, u32[]{:S(2)}) async-start(f32[32,1,4096]{2,1,0:T(1,128)} %reshape.1291), calls=%async_computation.11 | async-start | bytes 1048576 | tf_op jit(solution)/shard_map/all_to_all | solution.py:76
  636.6 7.2 copy-start.9
  659.4 25.1 %all-to-all-start.12 = ((f32[32,1,4096]{2,1,0:T(1,128)}), f32[32,1,4096]{2,1,0:T(1,128)}, u32[]{:S(2)}, u32[]{:S(2)}) async-start(f32[32,1,4096]{2,1,0:T(1,128)} %reshape.1293), calls=%async_computation.12 | async-start | bytes 1048576 | tf_op jit(solution)/shard_map/all_to_all | solution.py:75
  684.5 22.1 %all-to-all-start.13 = ((f32[32,1,4096]{2,1,0:T(1,128)}), f32[32,1,4096]{2,1,0:T(1,128)}, u32[]{:S(2)}, u32[]{:S(2)}) async-start(f32[32,1,4096]{2,1,0:T(1,128)} %reshape.1295), calls=%async_computation.13 | async-start | bytes 1048576 | tf_op jit(solution)/shard_map/all_to_all | solution.py:76
  731.2 5.1 copy-start.23
  757.0 7.0 copy-start.8
  779.8 69.1 %all-to-all-start.14 = ((f32[32,1,4096]{2,1,0:T(1,128)}), f32[32,1,4096]{2,1,0:T(1,128)}, u32[]{:S(2)}, u32[]{:S(2)}) async-start(f32[32,1,4096]{2,1,0:T(1,128)} %reshape.1297), calls=%async_computation.14 | async-start | bytes 1048576 | tf_op jit(solution)/shard_map/all_to_all | solution.py:75
  848.9 20.5 %all-to-all-start.15 = ((f32[32,1,4096]{2,1,0:T(1,128)}), f32[32,1,4096]{2,1,0:T(1,128)S(1)}, u32[]{:S(2)}, u32[]{:S(2)}) async-start(f32[32,1,4096]{2,1,0:T(1,128)} %reshape.1299), calls=%async_computation.15 | async-start | bytes 1048576 | tf_op jit(solution)/shard_map/all_to_all | solution.py:76
  (30 other events, 62.3 us)
where the time goes:
time: 894 us; the launch traced here: 883 us
  matrix products  321 us (36%)
  other arithmetic  217 us (24%)
  local copies, waits for them, and re-layouts  176 us (20%)
  starting transfers between devices  83.1 us (9%)
  blocking collectives  40.5 us (5%)
  waiting for transfers between devices  40.4 us (5%)
    unnamed x16, other arithmetic  167 us
    dot_general x29, matrix products, complex_einsum(): imag_term = jnp.einsum(formula, left_real, table_pair[1], precision=highest)  81.2 us
    dot_general x29, matrix products, complex_einsum(): real_term = jnp.einsum(formula, left_real, table_pair[0], precision=highest)  80 us
    unnamed x115, local copies, waits for them, and re-layouts  74.6 us
    dot_general x26, matrix products, complex_einsum(): jnp.einsum(formula, left_imag, table_pair[1], precision=highest)  74.2 us
    dot_general x26, matrix products, complex_einsum(): jnp.einsum(formula, left_imag, table_pair[0], precision=highest)  73.5 us
    all_to_all x8, starting transfers between devices, regroup(): lax.all_to_all(imag_part, ('px', 'py'), split_axis=2, concat_axis=1, tile...  49.1 us
    psum x1, blocking collectives, per_device(): total = lax.psum(0.5 * jnp.sum(residual * residual), ('px', 'py'))  40.5 us
  transfers between devices with their start and end apart: 16, of which 8 were waited for; matrix products, arithmetic and copies ran while one was open for 28% of the time, Pallas kernels for 0%

commit v1 on v0

v1 whole, which is shorter than its diff:
```python
import functools
import math

import jax
import jax.numpy as jnp
import numpy as np
from jax import lax
from jax.experimental import pallas as pl
from jax.experimental.pallas import tpu as pltpu
from jax.sharding import PartitionSpec as P

time_step = 0.25
axes = ("px", "py")
TILE = 128


def split_length(length):
    inner = 256 if length % 256 == 0 else TILE
    return (length // inner, inner)


def small_dft(items, sign):
    count = len(items)
    if count == 1:
        return items
    evens = small_dft(items[0::2], sign)
    odds = small_dft(items[1::2], sign)
    low, high = [], []
    for k in range(count // 2):
        odd_re, odd_im = odds[k]
        if 4 * k == count:
            odd_re, odd_im = (-odd_im, odd_re) if sign > 0 else (odd_im, -odd_re)
        elif k:
            c = math.cos(2.0 * math.pi * k / count)
            s = sign * math.sin(2.0 * math.pi * k / count)
            if abs(abs(c) - abs(s)) < 1e-12:
                sc, ss = math.copysign(1.0, c), math.copysign(1.0, s)
                odd_re, odd_im = (
                    c * (odd_re - sc * ss * odd_im),
                    c * (odd_im + sc * ss * odd_re),
                )
            else:
                odd_re, odd_im = (c * odd_re - s * odd_im, c * odd_im + s * odd_re)
        even_re, even_im = evens[k]
        low.append((even_re + odd_re, even_im + odd_im))
        high.append((even_re - odd_re, even_im - odd_im))
    return low + high


def halves(value):
    top = value.astype(jnp.bfloat16)
    return top, (value - top.astype(jnp.float32)).astype(jnp.bfloat16)


def tables(length):
    outer, inner = split_length(length)
    angle = 2.0 * np.pi * np.outer(np.arange(outer), np.arange(inner)) / length
    twiddle = np.stack([np.cos(angle), np.sin(angle)]) / math.sqrt(length)
    angle = 2.0 * np.pi * (np.outer(np.arange(inner), np.arange(inner)) % inner) / inner
    c, s = np.cos(angle), np.sin(angle)
    both = []
    for sign in (-1.0, 1.0):
        full = np.block([[c, sign * s], [-sign * s, c]])
        top = full.astype(jnp.bfloat16)
        low = (full - top.astype(np.float64)).astype(jnp.bfloat16)
        both.append(np.stack([top, low]))
    return twiddle.astype(np.float32), np.stack(both)


class Pieces:
    def __init__(self, length, rows, twiddle, matrix, turned, top, low, grid_out):
        self.length, self.rows = length, rows
        self.outer, self.inner = split_length(length)
        self.twiddle, self.matrix = twiddle, matrix
        self.turned, self.top, self.low, self.z = turned, top, low, grid_out
        self.step = math.gcd(rows, 16)

    def chunks(self, body):
        def run(i, carry):
            body(pl.multiple_of(i * self.step, self.step))
            return carry

        lax.fori_loop(0, self.rows // self.step, run, 0)

    def put(self, k, at, part, value):
        lanes = pl.ds(part * self.inner, self.inner)
        top, low = halves(value)
        self.top[k, at, lanes] = top
        self.low[k, at, lanes] = low

    def get(self, k, at, part):
        return self.z[k, at, pl.ds(part * self.inner, self.inner)]

    def multiply(self, sign, real_in=False, real_out=False):
        which = 0 if sign < 0 else 1
        deep = self.inner if real_in else 2 * self.inner
        wide = self.inner if real_out else 2 * self.inner
        count = self.outer * self.rows
        top = self.top[:, :, :deep].reshape(count, deep)
        low = self.low[:, :, :deep].reshape(count, deep)
        right_top = self.matrix[which, 0, :deep, :wide]
        right_low = self.matrix[which, 1, :deep, :wide]
        dot = functools.partial(jnp.dot, preferred_element_type=jnp.float32)
        total = dot(top, right_top) + dot(low, right_top) + dot(top, right_low)
        self.z[:, :, :wide] = total.reshape(self.outer, self.rows, wide)

    def twist(self, k, pair, sign):
        c = self.twiddle[0, pl.ds(k, 1), :]
        s = self.twiddle[1, pl.ds(k, 1), :]
        s = s if sign > 0 else -s
        re, im = pair
        return (re * c - im * s, re * s + im * c)

    def incoming(self, source, sign, real_out=False):
        rows, blocks = self.rows, max(TILE // self.rows, 1)
        span = blocks * rows
        for t in range(self.length // span):
            tile = source[pl.ds(t * blocks, blocks), :rows, :].reshape(span, 2 * rows)
            self.turned[: 2 * rows, pl.ds(t * span, span)] = tile.T

        def body(r0):
            items = []
            for j in range(self.outer):
                lanes = pl.ds(j * self.inner, self.inner)
                items.append((
                    self.turned[pl.ds(r0, self.step), lanes],
                    self.turned[pl.ds(rows + r0, self.step), lanes],
                ))
            for k, pair in enumerate(small_dft(items, sign)):
                re, im = self.twist(k, pair, sign)
                self.put(k, pl.ds(r0, self.step), 0, re)
                self.put(k, pl.ds(r0, self.step), 1, im)

        self.chunks(body)
        self.multiply(sign, real_out=real_out)

    def outgoing(self, sign, real_in, result):
        self.multiply(sign, real_in=real_in)
        rows = self.rows

        def body(r0):
            at = pl.ds(r0, self.step)
            items = [
                self.twist(k, (self.get(k, at, 0), self.get(k, at, 1)), sign)
                for k in range(self.outer)
            ]
            for j, (re, im) in enumerate(small_dft(items, sign)):
                for piece in range(self.inner // rows):
                    to = j * (self.inner // rows) + piece
                    lanes = slice(piece * rows, (piece + 1) * rows)
                    result[to, at, pl.ds(0, rows)] = re[:, lanes]
                    result[to, at, pl.ds(rows, rows)] = im[:, lanes]

        self.chunks(body)

    def spread(self, first, second, strided, result):
        rows, fill = self.rows, TILE - 2 * self.rows
        for t in range(self.length // TILE):
            lanes = pl.ds(t * TILE, TILE)
            parts = [first[:, lanes], second[:, lanes]]
            if fill:
                parts.append(jnp.zeros((fill, TILE), jnp.float32))
            strided[pl.ds(t * TILE, TILE), :] = jnp.concatenate(parts, axis=0).T
        for k in range(self.outer):
            slab = strided[pl.ds(k, self.inner, stride=self.outer), :].T
            result[k] = slab[: 2 * rows, :]

    def collect(self, slabs, strided, results):
        rows = self.rows
        for k in range(self.outer):
            slab = slabs(k)
            fill = TILE - slab.shape[0]
            if fill:
                slab = jnp.concatenate([slab, jnp.zeros((fill, self.inner), jnp.float32)], axis=0)
            strided[pl.ds(k, self.inner, stride=self.outer), :] = slab.T
        for t in range(self.length // TILE):
            block = strided[pl.ds(t * TILE, TILE), :].T
            for i, result in enumerate(results):
                result[:, pl.ds(t * TILE, TILE)] = block[i * rows : (i + 1) * rows, :]


def signed_waves(position, count):
    signed = jnp.where(position < count // 2, position, position - count)
    waves = 4.0 * signed.astype(jnp.float32) / count
    return waves, jnp.where(position == count // 2, jnp.float32(0.0), waves)


def wave_grids(piece, device, r0, k):
    shape = (piece.step, piece.inner)
    first = piece.outer * lax.broadcasted_iota(jnp.int32, (1, piece.inner), 1) + k
    second = device * piece.rows + r0 + lax.broadcasted_iota(jnp.int32, shape, 0)
    wave_first, deriv_first = signed_waves(first, piece.length)
    wave_second, deriv_second = signed_waves(second, piece.length)
    square = wave_first * wave_first + wave_second * wave_second
    denominator = 1.0 + time_step * (square * square - square)
    return deriv_first, deriv_second, denominator


def start_kernel(length, rows, field, target, twiddle, matrix, out, target_p, turned, top, low, z, strided):
    piece = Pieces(length, rows, twiddle, matrix, turned, top, low, z)
    piece.spread(field, target, strided, target_p)

    def body(r0):
        for k in range(piece.outer):
            piece.put(k, pl.ds(r0, piece.step), 0, target_p[k, pl.ds(r0, piece.step), :])

    piece.chunks(body)
    piece.outgoing(-1.0, True, out)


def spread_kernel(length, rows, forcing, result, strided):
    piece = Pieces(length, rows, None, None, None, None, None, None)
    piece.spread(forcing.at[0], forcing.at[1], strided, result)


def collect_kernel(length, rows, slabs, result, strided):
    piece = Pieces(length, rows, None, None, None, None, None, None)
    piece.collect(lambda k: slabs[k], strided, [result.at[i] for i in range(result.shape[0])])


def spectral_kernel(kind, length, rows, *refs):
    device_ref, source, *rest = refs
    device = device_ref[0]
    if kind == "slope":
        twiddle, matrix, out, state_out, *scratch = rest
    elif kind == "next":
        state_in, forcing_in, twiddle, matrix, out, *scratch = rest
    elif kind == "misfit":
        twiddle, matrix, out, coef_out, total_out, *scratch = rest
    else:
        coef_in, twiddle, matrix, out, *scratch = rest
    piece = Pieces(length, rows, twiddle, matrix, *scratch[:4])
    piece.incoming(source, -1.0)

    def body(r0):
        at = pl.ds(r0, piece.step)
        also = pl.ds(rows + r0, piece.step)
        for k in range(piece.outer):
            re, im = piece.get(k, at, 0), piece.get(k, at, 1)
            deriv_first, deriv_second, denominator = wave_grids(piece, device, r0, k)
            if kind == "slope":
                state_out[k, at, :], state_out[k, also, :] = re, im
                new_re = -deriv_first * im - deriv_second * re
                new_im = deriv_first * re - deriv_second * im
            elif kind == "next":
                inverse = 1.0 / denominator
                new_re = (state_in[k, at, :] + time_step * (re + forcing_in[k, at, :])) * inverse
                new_im = (state_in[k, also, :] + time_step * (im + forcing_in[k, also, :])) * inverse
            elif kind == "misfit":
                inverse = 1.0 / denominator
                new_re, new_im = time_step * (re * inverse), time_step * (im * inverse)
                coef_out[k, at, :], coef_out[k, also, :] = new_re, new_im
            else:
                scale = 1.0 / time_step
                new_re = scale * coef_in[k, at, :] - deriv_first * im + deriv_second * re
                new_im = scale * coef_in[k, also, :] + deriv_first * re + deriv_second * im
            piece.put(k, at, 0, new_re)
            piece.put(k, at, 1, new_im)

    piece.chunks(body)
    piece.outgoing(1.0, False, out)
    if kind == "misfit":
        total_out[...] = jnp.sum(source[:, pl.ds(rows, 8), :], axis=0)


def physical_kernel(kind, length, rows, *refs):
    source, *rest = refs
    if kind == "nonlinear":
        twiddle, matrix, out, grads_out, *scratch = rest
    elif kind == "residual":
        target_p, twiddle, matrix, out, field_out, *scratch = rest
    elif kind == "joint":
        grads_in, twiddle, matrix, out, *scratch = rest
    else:
        twiddle, matrix, field_out, *scratch = rest
    piece = Pieces(length, rows, twiddle, matrix, *scratch[:4])
    piece.incoming(source, 1.0, real_out=kind != "nonlinear")
    if kind in ("residual", "last"):
        piece.collect(lambda k: piece.get(k, pl.ds(0, rows), 0), scratch[4], [field_out])
    if kind == "last":
        return
    if kind == "residual":
        total = scratch[5]
        total[...] = jnp.zeros_like(total)

    def body(r0):
        at = pl.ds(r0, piece.step)
        also = pl.ds(rows + r0, piece.step)
        for k in range(piece.outer):
            re = piece.get(k, at, 0)
            if kind == "nonlinear":
                im = piece.get(k, at, 1)
                grads_out[k, at, :], grads_out[k, also, :] = re, im
                piece.put(k, at, 0, -0.5 * (re * re + im * im))
            elif kind == "residual":
                residual = re - target_p[k, also, :]
                total[...] += residual * residual
                piece.put(k, at, 0, residual)
            else:
                piece.put(k, at, 0, re * grads_in[k, at, :])
                piece.put(k, at, 1, re * grads_in[k, also, :])

    piece.chunks(body)
    piece.outgoing(-1.0, kind != "joint", out)
    if kind == "residual":
        value = 0.5 * jnp.sum(total[...])
        out[:, pl.ds(rows, 8), :] = jnp.full((out.shape[0], 8, 2 * rows), value, jnp.float32)


def member_step(device, field, target, forcing_p, constants, devices, rows, length):
    outer, inner = split_length(length)
    float32 = jnp.float32
    blocks = jax.ShapeDtypeStruct((devices, rows, 2 * rows), float32)
    longer = jax.ShapeDtypeStruct((devices, rows + 8, 2 * rows), float32)
    pair = jax.ShapeDtypeStruct((outer, 2 * rows, inner), float32)
    plain = jax.ShapeDtypeStruct((rows, length), float32)
    step = math.gcd(rows, 16)
    base = [
        pltpu.VMEM((2 * rows, length), float32),
        pltpu.VMEM((outer, rows, 2 * inner), jnp.bfloat16),
        pltpu.VMEM((outer, rows, 2 * inner), jnp.bfloat16),
        pltpu.VMEM((outer, rows, 2 * inner), float32),
    ]
    strided = pltpu.VMEM((length, TILE), float32)
    total = pltpu.VMEM((step, inner), float32)
    vmem = pl.BlockSpec(memory_space=pltpu.VMEM)
    smem = pl.BlockSpec(memory_space=pltpu.SMEM)

    def call(body, outs, scratch, *operands, scalar=False):
        specs = [smem if scalar and i == 0 else vmem for i in range(len(operands))]
        return pl.pallas_call(
            functools.partial(body, length, rows),
            out_shape=outs,
            in_specs=specs,
            out_specs=jax.tree.map(lambda leaf: vmem, outs),
            scratch_shapes=scratch,
            compiler_params=pltpu.CompilerParams(vmem_limit_bytes=48 * 2**20),
        )(*operands)

    def move(value):
        return lax.all_to_all(value, axes, split_axis=0, concat_axis=0, tiled=True)

    spectral = lambda kind: functools.partial(spectral_kernel, kind)
    physical = lambda kind: functools.partial(physical_kernel, kind)
    sent, target_p = call(start_kernel, (blocks, pair), base + [strided], field, target, *constants)
    sent, state = call(spectral("slope"), (blocks, pair), base, device, move(sent), *constants, scalar=True)
    sent, grads = call(physical("nonlinear"), (blocks, pair), base, move(sent), *constants)
    sent = call(spectral("next"), blocks, base, device, move(sent), state, forcing_p, *constants, scalar=True)
    sent, next_field = call(
        physical("residual"), (longer, plain), base + [strided, total], move(sent), target_p, *constants
    )
    sent, coef, sums = call(
        spectral("misfit"),
        (blocks, pair, jax.ShapeDtypeStruct((8, 2 * rows), float32)),
        base, device, move(sent), *constants, scalar=True,
    )
    sent = call(physical("joint"), blocks, base, move(sent), grads, *constants)
    sent = call(spectral("total"), blocks, base, device, move(sent), coef, *constants, scalar=True)
    field_grad = call(physical("last"), plain, base + [strided], move(sent), *constants)
    return next_field, sums[0, 0], field_grad, coef


def per_device(devices, initial_field, target_field, forcing):
    members, rows, length = initial_field.shape
    device = lax.axis_index(axes).astype(jnp.int32).reshape(1)
    constants = [jnp.asarray(table) for table in tables(length)]
    outer, inner = split_length(length)
    vmem = pl.BlockSpec(memory_space=pltpu.VMEM)
    strided = pltpu.VMEM((length, TILE), jnp.float32)

    def reorder(body, shape, operand):
        return pl.pallas_call(
            functools.partial(body, length, rows),
            out_shape=jax.ShapeDtypeStruct(shape, jnp.float32),
            in_specs=[vmem],
            out_specs=vmem,
            scratch_shapes=[strided],
        )(operand)

    forcing_p = reorder(spread_kernel, (outer, 2 * rows, inner), forcing)
    results = [
        member_step(device, initial_field[m], target_field[m], forcing_p, constants, devices, rows, length)
        for m in range(members)
    ]
    next_field = jnp.stack([one[0] for one in results])
    objective = sum(one[1] for one in results) / (members * length * length)
    field_grad = jnp.stack([one[2] for one in results])
    forcing_grad = reorder(collect_kernel, (2, rows, length), sum(one[3] for one in results))
    return (next_field, objective, field_grad, forcing_grad)


def solution(mesh):
    devices = mesh.shape["px"] * mesh.shape["py"]
    spec = P(None, axes, None)
    return jax.shard_map(
        functools.partial(per_device, devices),
        mesh=mesh,
        in_specs=(spec, spec, spec),
        out_specs=(spec, P(), spec, spec),
        check_vma=False,
    )
```

time: 894 us -> 291 us (0.33); the launches traced: 883 us -> 290 us
  matrix products: 321 us -> 0 us
  other arithmetic: 217 us -> 0 us
  local copies, waits for them, and re-layouts: 176 us -> 11.1 us
  blocking collectives: 40.5 us -> 151 us
  starting transfers between devices: 83.1 us -> 14.6 us
  Pallas kernels: 0 us -> 39.3 us
  waiting for transfers between devices: 40.4 us -> 71.6 us
    dot_general x116 -> x0, matrix products: 321 us -> none  [the longest x29 81.2 us: complex_einsum(): imag_term = jnp.einsum(formula, left_real, table_pair[1], precision=highest)]
    unnamed x16 -> x0, other arithmetic: 167 us -> none
    all_to_all x0 -> x5, blocking collectives: none -> 151 us  [move(): return lax.all_to_all(value, axes, split_axis=0, concat_axis=0, tiled=True)]
    all_to_all x16 -> x3, starting transfers between devices: 83.1 us -> 14.6 us  [move(): return lax.all_to_all(value, axes, split_axis=0, concat_axis=0, tiled=True)]
    unnamed x115 -> x32, local copies, waits for them, and re-layouts: 74.6 us -> 10.6 us
    all_to_all x16 -> x0, other arithmetic: 40.7 us -> none  [the longest x8 20.9 us: regroup(): lax.all_to_all(real_part, ('px', 'py'), split_axis=2, concat_axis=1, tile...]
    psum x1 -> x0, blocking collectives: 40.5 us -> none  [per_device(): total = lax.psum(0.5 * jnp.sum(residual * residual), ('px', 'py'))]
    pallas_call x0 -> x11, Pallas kernels: none -> 39.3 us  [the longest x9 33.4 us: call(): pl.pallas_call(functools.partial(body, length, rows), out_shape=outs, in_...]
  transfers between devices with their start and end apart: 16 -> 3, of which waited for: 8 -> 3; matrix products, arithmetic and copies ran while one was open for 28% -> 0% of each run, Pallas kernels for 0% -> 2%
where the time goes in v1:
time: 291 us; the launch traced here: 290 us
  blocking collectives  151 us (52%)
  waiting for transfers between devices  71.6 us (25%)
  Pallas kernels  39.3 us (14%)
  starting transfers between devices  14.6 us (5%)
  local copies, waits for them, and re-layouts  11.1 us (4%)
    all_to_all x5, blocking collectives, move(): return lax.all_to_all(value, axes, split_axis=0, concat_axis=0, tiled=True)  151 us
    all_to_all x3, waiting for transfers between devices, move(): return lax.all_to_all(value, axes, split_axis=0, concat_axis=0, tiled=True)  71.6 us
    pallas_call x9, Pallas kernels, call(): pl.pallas_call(functools.partial(body, length, rows), out_shape=outs, in_...  33.4 us
    all_to_all x3, starting transfers between devices, move(): return lax.all_to_all(value, axes, split_axis=0, concat_axis=0, tiled=True)  14.6 us
    unnamed x32, local copies, waits for them, and re-layouts  10.6 us
    pallas_call x2, Pallas kernels, reorder(): pl.pallas_call(functools.partial(body, length, rows), out_shape=jax.Shape...  5.83 us
  transfers between devices with their start and end apart: 3, of which 3 were waited for; matrix products, arithmetic and copies ran while one was open for 0% of the time, Pallas kernels for 2%

profile of v1, /device:TPU:0, one launch (start us, length us, event | category | flops | bytes accessed | tf_op | source)
XLA Modules:
  0.0 290.0 jit_solution(4243013599942937062)
XLA Ops:
  0.6 1.6 copy-done
  5.0 2.0 shard_map.84
  9.1 7.3 %all-to-all-start = ((f32[32,64,128]{2,1,0:T(8,128)}), f32[32,64,128]{2,1,0:T(8,128)S(1)}, u32[]{:S(2)}, u32[]{:S(2)}) async-start(f32[32,64,128]{2,1,0:T(8,128)} %copy-done.10), calls=%async_computation | async-start | bytes 2097152 | tf_op jit(solution)/shard_map/all_to_all | solution.py:341
  16.4 26.2 %all-to-all-done.refs_1_ = f32[32,64,128]{2,1,0:T(8,128)S(1)} async-done(((f32[32,64,128]{2,1,0:T(8,128)}), f32[32,64,128]{2,1,0:T(8,128)S(1)}, u32[]{:S(2)}, u32[]{:S(2)}) %all-to-all-start) | async-done | bytes 1048608 | tf_op jit(solution)/shard_map/all_to_all | solution.py:341
  42.6 3.8 %shard_map.85 = (f32[32,64,128]{2,1,0:T(8,128)S(1)}, f32[8,128,256]{2,1,0:T(8,128)S(1)}) custom-call(s32[1]{0:T(128)} %bitcast.refs_0_, f32[32,64,128]{2,1,0:T(8,128)S(1)} %all-to-all-done.refs_1_, f32[2,8,256]{2,1,0:T(8,128)S(1)} %copy-done.7, bf16[2,2,512,512]{3,2,1,0:T(8,128)(2,1)S(1)} %copy-done.1), custom_call_target="tpu_custom_call" | custom-call | tf_op jit(solution)/shard_map/pallas_call | solution.py:331
  47.4 29.6 %all_to_all.40.refs_0_ = f32[32,64,128]{2,1,0:T(8,128)S(1)} all-to-all(f32[32,64,128]{2,1,0:T(8,128)S(1)} %get-tuple-element.16), channel_id=1, replica_groups=mesh['px'=8,'py'=4] {'px','py'}, dimensions={0} | all-to-all | bytes 2097152 | tf_op jit(solution)/shard_map/all_to_all | solution.py:341
  77.0 3.2 %shard_map.86 = (f32[32,64,128]{2,1,0:T(8,128)S(1)}, f32[8,128,256]{2,1,0:T(8,128)S(1)}) custom-call(f32[32,64,128]{2,1,0:T(8,128)S(1)} %all_to_all.40.refs_0_, f32[2,8,256]{2,1,0:T(8,128)S(1)} %copy-done.7, bf16[2,2,512,512]{3,2,1,0:T(8,128)(2,1)S(1)} %copy-done.1), custom_call_target="tpu_custom_call" | custom-call | tf_op jit(solution)/shard_map/pallas_call | solution.py:331
  81.1 3.6 %all-to-all-start.2 = ((f32[32,64,128]{2,1,0:T(8,128)}), f32[32,64,128]{2,1,0:T(8,128)S(1)}, u32[]{:S(2)}, u32[]{:S(2)}) async-start(f32[32,64,128]{2,1,0:T(8,128)} %copy-done.11), calls=%async_computation.2 | async-start | bytes 2097152 | tf_op jit(solution)/shard_map/all_to_all | solution.py:341
  84.7 3.0 %shard_map.87.refs_3_ = f32[8,128,256]{2,1,0:T(8,128)} custom-call(f32[2,64,2048]{2,1,0:T(8,128)} %forcing.1), custom_call_target="tpu_custom_call" | custom-call | tf_op jit(solution)/shard_map/pallas_call | solution.py:372
  87.7 23.2 %all-to-all-done.2.refs_1_ = f32[32,64,128]{2,1,0:T(8,128)S(1)} async-done(((f32[32,64,128]{2,1,0:T(8,128)}), f32[32,64,128]{2,1,0:T(8,128)S(1)}, u32[]{:S(2)}, u32[]{:S(2)}) %all-to-all-start.2) | async-done | bytes 1048608 | tf_op jit(solution)/shard_map/all_to_all | solution.py:341
  110.9 1.2 copy-done.3
  112.2 5.5 %shard_map.88 = f32[32,64,128]{2,1,0:T(8,128)S(1)} custom-call(s32[1]{0:T(128)} %bitcast.refs_0_, f32[32,64,128]{2,1,0:T(8,128)S(1)} %all-to-all-done.2.refs_1_, f32[8,128,256]{2,1,0:T(8,128)S(1)} %copy-done.9, f32[8,128,256]{2,1,0:T(8,128)S(1)} %copy-done.3, f32[2,8,256]{2,1,0:T(8,128)S(1)} %copy-done.7, ...), custom_call_target="tpu_custom_call" | custom-call | tf_op jit(solution)/shard_map/pallas_call | solution.py:331
  117.7 29.6 %all_to_all.41.refs_0_ = f32[32,64,128]{2,1,0:T(8,128)S(1)} all-to-all(f32[32,64,128]{2,1,0:T(8,128)S(1)} %shard_map.88), channel_id=1, replica_groups=mesh['px'=8,'py'=4] {'px','py'}, dimensions={0} | all-to-all | bytes 2097152 | tf_op jit(solution)/shard_map/all_to_all | solution.py:341
  147.4 4.7 %shard_map.89 = (f32[32,72,128]{2,1,0:T(8,128)S(1)}, f32[64,2048]{1,0:T(8,128)}) custom-call(f32[32,64,128]{2,1,0:T(8,128)S(1)} %all_to_all.41.refs_0_, f32[8,128,256]{2,1,0:T(8,128)S(1)} %copy-done.13, f32[2,8,256]{2,1,0:T(8,128)S(1)} %copy-done.7, bf16[2,2,512,512]{3,2,1,0:T(8,128)(2,1)S(1)} %copy-done.2), custom_call_target="tpu_custom_call" | custom-call | tf_op jit(solution)/shard_map/pallas_call | solution.py:331
  152.1 34.0 %all_to_all.42.refs_1_ = f32[32,72,128]{2,1,0:T(8,128)S(1)} all-to-all(f32[32,72,128]{2,1,0:T(8,128)S(1)} %get-tuple-element.21), channel_id=1, replica_groups=mesh['px'=8,'py'=4] {'px','py'}, dimensions={0} | all-to-all | bytes 2359296 | tf_op jit(solution)/shard_map/all_to_all | solution.py:341
  186.1 3.9 %shard_map.90 = (f32[32,64,128]{2,1,0:T(8,128)S(1)}, f32[8,128,256]{2,1,0:T(8,128)S(1)}, f32[8,128]{1,0:T(8,128)S(1)}) custom-call(s32[1]{0:T(128)} %bitcast.refs_0_, f32[32,72,128]{2,1,0:T(8,128)S(1)} %all_to_all.42.refs_1_, f32[2,8,256]{2,1,0:T(8,128)S(1)} %copy-done.7, bf16[2,2,512,512]{3,2,1,0:T(8,128)(2,1)S(1)} %copy-done.2), custom_call_target="tpu_custom_call" | custom-call | tf_op jit(solution)/shard_map/pallas_call | solution.py:331
  190.0 28.0 %all_to_all.43.refs_0_ = f32[32,64,128]{2,1,0:T(8,128)S(1)} all-to-all(f32[32,64,128]{2,1,0:T(8,128)S(1)} %get-tuple-element.23), channel_id=1, replica_groups=mesh['px'=8,'py'=4] {'px','py'}, dimensions={0} | all-to-all | bytes 2097152 | tf_op jit(solution)/shard_map/all_to_all | solution.py:341
  218.0 3.9 %shard_map.91 = f32[32,64,128]{2,1,0:T(8,128)S(1)} custom-call(f32[32,64,128]{2,1,0:T(8,128)S(1)} %all_to_all.43.refs_0_, f32[8,128,256]{2,1,0:T(8,128)S(1)} %get-tuple-element.24.refs_1_, f32[2,8,256]{2,1,0:T(8,128)S(1)} %copy-done.7, bf16[2,2,512,512]{3,2,1,0:T(8,128)(2,1)S(1)} %copy-done.2), custom_call_target="tpu_custom_call" | custom-call | tf_op jit(solution)/shard_map/pallas_call | solution.py:331
  222.0 29.6 %all_to_all.44.refs_1_ = f32[32,64,128]{2,1,0:T(8,128)S(1)} all-to-all(f32[32,64,128]{2,1,0:T(8,128)S(1)} %shard_map.91), channel_id=1, replica_groups=mesh['px'=8,'py'=4] {'px','py'}, dimensions={0} | all-to-all | bytes 2097152 | tf_op jit(solution)/shard_map/all_to_all | solution.py:341
  251.6 3.8 %shard_map.92 = f32[32,64,128]{2,1,0:T(8,128)S(1)} custom-call(s32[1]{0:T(128)} %bitcast.refs_0_, f32[32,64,128]{2,1,0:T(8,128)S(1)} %all_to_all.44.refs_1_, f32[8,128,256]{2,1,0:T(8,128)S(1)} %get-tuple-element.25.refs_2_.slabs, f32[2,8,256]{2,1,0:T(8,128)S(1)} %copy-done.7, bf16[2,2,512,512]{3,2,1,0:T(8,128)(2,1)S(1)} %copy-done.2), custom_call_target="tpu_custom_call" | custom-call | tf_op jit(solution)/shard_map/pallas_call | solution.py:331
  256.4 3.6 %all-to-all-start.7 = ((f32[32,64,128]{2,1,0:T(8,128)}), f32[32,64,128]{2,1,0:T(8,128)S(1)}, u32[]{:S(2)}, u32[]{:S(2)}) async-start(f32[32,64,128]{2,1,0:T(8,128)} %copy-done.5), calls=%async_computation.7 | async-start | bytes 2097152 | tf_op jit(solution)/shard_map/all_to_all | solution.py:341
  260.0 2.9 shard_map.94
  264.1 22.2 %all-to-all-done.7.refs_0_ = f32[32,64,128]{2,1,0:T(8,128)S(1)} async-done(((f32[32,64,128]{2,1,0:T(8,128)}), f32[32,64,128]{2,1,0:T(8,128)S(1)}, u32[]{:S(2)}, u32[]{:S(2)}) %all-to-all-start.7) | async-done | bytes 1048608 | tf_op jit(solution)/shard_map/all_to_all | solution.py:341
  286.2 2.6 shard_map.93
  (31 shorter events, 8.3 us)
Async XLA Ops:
  0.6 1.6 copy-start
  2.2 0.7 copy-start.6
  2.9 1.0 copy-start.14
  4.0 1.0 copy-start.15
  7.1 1.0 copy-start.10
  8.0 1.0 copy-start.12
  9.1 33.5 %copy-start.1 = (bf16[2,2,512,512]{3,2,1,0:T(8,128)(2,1)S(1)}, bf16[2,2,512,512]{3,2,1,0:T(8,128)(2,1)}, u32[]{:S(2)}) copy-start(bf16[2,2,512,512]{3,2,1,0:T(8,128)(2,1)} %constant.20.clone.matrix.refs_3_.refs_2_.refs_5_.refs_4_) | copy-start | bytes 6291460
  9.1 33.5 %copy-start.7 = (f32[2,8,256]{2,1,0:T(8,128)S(1)}, f32[2,8,256]{2,1,0:T(8,128)}, u32[]{:S(2)}) copy-start(f32[2,8,256]{2,1,0:T(8,128)} %constant.19.clone.twiddle.refs_2_.refs_1_.refs_4_.refs_3_) | copy-start | bytes 49156
  9.1 33.5 %all-to-all-start = ((f32[32,64,128]{2,1,0:T(8,128)}), f32[32,64,128]{2,1,0:T(8,128)S(1)}, u32[]{:S(2)}, u32[]{:S(2)}) async-start(f32[32,64,128]{2,1,0:T(8,128)} %copy-done.10), calls=%async_computation | async-start | bytes 2097152 | tf_op jit(solution)/shard_map/all_to_all | solution.py:341
  46.4 1.0 copy-start.8
  80.1 1.0 copy-start.11
  81.1 29.8 %all-to-all-start.2 = ((f32[32,64,128]{2,1,0:T(8,128)}), f32[32,64,128]{2,1,0:T(8,128)S(1)}, u32[]{:S(2)}, u32[]{:S(2)}) async-start(f32[32,64,128]{2,1,0:T(8,128)} %copy-done.11), calls=%async_computation.2 | async-start | bytes 2097152 | tf_op jit(solution)/shard_map/all_to_all | solution.py:341
  84.7 26.2 %copy-start.9 = (f32[8,128,256]{2,1,0:T(8,128)S(1)}, f32[8,128,256]{2,1,0:T(8,128)}, u32[]{:S(2)}) copy-start(f32[8,128,256]{2,1,0:T(8,128)} %copy-done.8) | copy-start | bytes 3145732
  110.9 1.2 copy-start.3
  112.2 35.2 %copy-start.13 = (f32[8,128,256]{2,1,0:T(8,128)S(1)}, f32[8,128,256]{2,1,0:T(8,128)}, u32[]{:S(2)}) copy-start(f32[8,128,256]{2,1,0:T(8,128)} %copy-done.12) | copy-start | bytes 3145732
  117.7 29.6 %copy-start.2 = (bf16[2,2,512,512]{3,2,1,0:T(8,128)(2,1)S(1)}, bf16[2,2,512,512]{3,2,1,0:T(8,128)(2,1)}, u32[]{:S(2)}) copy-start(bf16[2,2,512,512]{3,2,1,0:T(8,128)(2,1)} %constant.20.clone.matrix.refs_3_.refs_2_.refs_5_.refs_4_) | copy-start | bytes 6291460
  190.0 61.6 %copy-start.4 = (f32[8,128,256]{2,1,0:T(8,128)}, f32[8,128,256]{2,1,0:T(8,128)S(1)}, u32[]{:S(2)}) copy-start(f32[8,128,256]{2,1,0:T(8,128)S(1)} %get-tuple-element.25.refs_2_.slabs) | copy-start | bytes 3145732
  255.4 1.0 copy-start.5
  256.4 29.8 %all-to-all-start.7 = ((f32[32,64,128]{2,1,0:T(8,128)}), f32[32,64,128]{2,1,0:T(8,128)S(1)}, u32[]{:S(2)}, u32[]{:S(2)}) async-start(f32[32,64,128]{2,1,0:T(8,128)} %copy-done.5), calls=%async_computation.7 | async-start | bytes 2097152 | tf_op jit(solution)/shard_map/all_to_all | solution.py:341

commit v2 on v1

v2 whole, which is shorter than its diff:
```python
import functools
import math

import jax
import jax.numpy as jnp
import numpy as np
from jax import lax
from jax.experimental import pallas as pl
from jax.experimental.pallas import tpu as pltpu
from jax.sharding import PartitionSpec as P

time_step = 0.25
axes = ("px", "py")
TILE = 128


def split_length(length):
    inner = 256 if length % 256 == 0 else TILE
    return (length // inner, inner)


def small_dft(items, sign):
    count = len(items)
    if count == 1:
        return items
    evens = small_dft(items[0::2], sign)
    odds = small_dft(items[1::2], sign)
    low, high = [], []
    for k in range(count // 2):
        odd_re, odd_im = odds[k]
        if 4 * k == count:
            odd_re, odd_im = (-odd_im, odd_re) if sign > 0 else (odd_im, -odd_re)
        elif k:
            c = math.cos(2.0 * math.pi * k / count)
            s = sign * math.sin(2.0 * math.pi * k / count)
            if abs(abs(c) - abs(s)) < 1e-12:
                sc, ss = math.copysign(1.0, c), math.copysign(1.0, s)
                odd_re, odd_im = (
                    c * (odd_re - sc * ss * odd_im),
                    c * (odd_im + sc * ss * odd_re),
                )
            else:
                odd_re, odd_im = (c * odd_re - s * odd_im, c * odd_im + s * odd_re)
        even_re, even_im = evens[k]
        low.append((even_re + odd_re, even_im + odd_im))
        high.append((even_re - odd_re, even_im - odd_im))
    return low + high


def halves(value):
    top = value.astype(jnp.bfloat16)
    return top, (value - top.astype(jnp.float32)).astype(jnp.bfloat16)


def orders(length, rows):
    inner = split_length(length)[1]
    half = rows // 2
    lane = np.arange(inner)
    natural = lane
    local = lane % (inner // 2)
    line = local % half
    kept = rows * (local // half) + np.where((lane >= inner // 2) & (line == 0), half, line)
    groups = TILE // rows
    tall = rows // groups
    within = lane % (inner // groups)
    lines = rows * (within // tall) + tall * (lane // (inner // groups)) + within % tall
    return natural, kept, lines


def twiddle_table(length, order):
    outer = split_length(length)[0]
    angle = 2.0 * np.pi * np.outer(np.arange(outer), order) / length
    return (np.stack([np.cos(angle), np.sin(angle)]) / math.sqrt(length)).astype(np.float32)


def matrix_table(length, sign, left, right):
    inner = split_length(length)[1]
    angle = 2.0 * np.pi * (np.outer(left, right) % inner) / inner
    c, s = np.cos(angle), np.sin(angle)
    full = np.block([[c, sign * s], [-sign * s, c]])
    top = full.astype(jnp.bfloat16)
    return np.stack([top, (full - top.astype(np.float64)).astype(jnp.bfloat16)])


def mirror_table(length):
    inner = split_length(length)[1]
    lane = np.arange(inner)
    both = np.zeros((2, inner, inner))
    both[0, (inner - lane) % inner, lane] = 1.0
    both[1, inner - 1 - lane, lane] = 1.0
    return both.astype(jnp.bfloat16)


class Pieces:
    def __init__(self, length, rows, turned=None, top=None, low=None, grid_out=None):
        self.length, self.rows, self.half = length, rows, rows // 2
        self.outer, self.inner = split_length(length)
        self.turned, self.top, self.low, self.z = turned, top, low, grid_out
        self.step = math.gcd(rows // 2, 16)

    def chunks(self, lines, body):
        def run(i, carry):
            body(pl.multiple_of(i * self.step, self.step))
            return carry

        lax.fori_loop(0, lines // self.step, run, 0)

    def put(self, k, at, part, value):
        lanes = pl.ds(part * self.inner, self.inner)
        top, low = halves(value)
        self.top[k, at, lanes] = top
        self.low[k, at, lanes] = low

    def get(self, k, at, part):
        return self.z[k, at, pl.ds(part * self.inner, self.inner)]

    def multiply(self, lines, matrix, real_in=False, real_out=False):
        deep = self.inner if real_in else 2 * self.inner
        wide = self.inner if real_out else 2 * self.inner
        count = self.outer * lines
        top = self.top[:, :lines, :deep].reshape(count, deep)
        low = self.low[:, :lines, :deep].reshape(count, deep)
        right_top = matrix[0, :deep, :wide]
        right_low = matrix[1, :deep, :wide]
        dot = functools.partial(jnp.dot, preferred_element_type=jnp.float32)
        total = dot(top, right_top) + dot(low, right_top) + dot(top, right_low)
        self.z[:, :lines, :wide] = total.reshape(self.outer, lines, wide)

    def twist(self, k, pair, sign, twiddle):
        c = twiddle[0, pl.ds(k, 1), :]
        s = twiddle[1, pl.ds(k, 1), :]
        s = s if sign > 0 else -s
        re, im = pair
        return (re * c - im * s, re * s + im * c)

    def turn_full(self, source):
        rows, blocks = self.rows, TILE // self.rows
        for t in range(self.length // TILE):
            tile = source[pl.ds(t * blocks, blocks), :rows, :].reshape(TILE, 2 * rows)
            self.turned[: 2 * rows, pl.ds(t * TILE, TILE)] = tile.T

    def turn_lines(self, source):
        rows = self.rows
        groups = TILE // rows
        blocks, wide = self.inner // rows, self.inner // groups
        for t in range(self.outer):
            tile = source[pl.ds(t * blocks, blocks), :, :].reshape(wide, TILE).T
            for h in range(groups):
                self.turned[:rows, pl.ds(t * self.inner + h * wide, wide)] = tile[h * rows : (h + 1) * rows]

    def kept_lanes(self, j):
        wide = self.inner // 2
        return j * self.inner + (wide if 2 * j >= self.outer else 0), wide

    def clear_other(self, j):
        at, wide = self.kept_lanes(j)
        other = j * self.inner + (0 if 2 * j >= self.outer else wide)
        self.turned[: 2 * self.rows, pl.ds(other, wide)] = jnp.zeros((2 * self.rows, wide), jnp.float32)

    def turn_kept(self, source):
        rows, half, blocks = self.rows, self.half, self.inner // self.rows
        for j in range(self.outer):
            at, wide = self.kept_lanes(j)
            tile = source[pl.ds(j * blocks, blocks), :, :].reshape(wide, 2 * rows)
            self.turned[: 2 * rows, pl.ds(at, wide)] = tile.T
            self.clear_other(j)

    def unpack_middle(self):
        rows, middle = self.rows, (self.outer // 2) * self.inner
        first = self.turned[rows : 2 * rows, :TILE]
        lane0 = lax.broadcasted_iota(jnp.int32, first.shape, 1) == 0
        zero = jnp.zeros_like(first)
        self.turned[:rows, pl.ds(middle, TILE)] += jnp.where(lane0, first, zero)
        self.turned[rows : 2 * rows, :TILE] = jnp.where(lane0, zero, first)

    def incoming(self, lines, sign, twiddle, matrix, real_out=False):
        def body(r0):
            items = []
            for j in range(self.outer):
                lanes = pl.ds(j * self.inner, self.inner)
                items.append((
                    self.turned[pl.ds(r0, self.step), lanes],
                    self.turned[pl.ds(lines + r0, self.step), lanes],
                ))
            for k, pair in enumerate(small_dft(items, sign)):
                re, im = self.twist(k, pair, sign, twiddle)
                self.put(k, pl.ds(r0, self.step), 0, re)
                self.put(k, pl.ds(r0, self.step), 1, im)

        self.chunks(lines, body)
        self.multiply(lines, matrix, real_out=real_out)

    def outgoing(self, lines, sign, twiddle, matrix, real_in, write):
        self.multiply(lines, matrix, real_in=real_in)

        def body(r0):
            at = pl.ds(r0, self.step)
            write(r0, small_dft([
                self.twist(k, (self.get(k, at, 0), self.get(k, at, 1)), sign, twiddle)
                for k in range(self.outer)
            ], sign))

        self.chunks(lines, body)

    def pack_middle(self, items):
        re, im = items[0]
        lane0 = lax.broadcasted_iota(jnp.int32, im.shape, 1) == 0
        return [(re, jnp.where(lane0, items[self.outer // 2][0], im))] + items[1:]

    def write_full(self, result, pack):
        rows = self.rows

        def write(r0, items):
            at = pl.ds(r0, self.step)
            for j, (re, im) in enumerate(self.pack_middle(items) if pack else items):
                for piece in range(self.inner // rows):
                    to = j * (self.inner // rows) + piece
                    lanes = slice(piece * rows, (piece + 1) * rows)
                    result[to, at, pl.ds(0, rows)] = re[:, lanes]
                    result[to, at, pl.ds(rows, rows)] = im[:, lanes]

        return write

    def outgoing_kept(self, twiddle, matrix, result):
        self.multiply(self.rows, matrix, real_in=True)
        rows, half, blocks = self.rows, self.half, self.inner // self.rows
        tall = rows * rows // TILE
        step = math.gcd(rows, 16)
        span = min(tall, step)
        for h in range(rows // max(tall, step)):

            def body(i, carry, h=h):
                r0 = i * step if isinstance(i, int) else pl.multiple_of(i * step, step)
                at = pl.ds(h * max(tall, step) + r0, step)
                items = self.pack_middle(small_dft([
                    self.twist(k, (self.get(k, at, 0), self.get(k, at, 1)), -1.0, twiddle)
                    for k in range(self.outer)
                ], -1.0))
                for j, pair in enumerate(items):
                    base = self.inner // 2 if 2 * j >= self.outer else 0
                    for piece in range(blocks):
                        lanes = slice(base + piece * half, base + (piece + 1) * half)
                        for part, value in enumerate(pair):
                            for sub in range(step // span):
                                group = h * (step // span) + sub
                                to = pl.ds(group * rows + part * half, half)
                                held = value[sub * span : (sub + 1) * span, lanes]
                                result[j * blocks + piece, pl.ds(r0, span), to] = held
                return carry

            if tall > step:
                lax.fori_loop(0, tall // step, body, 0)
            else:
                body(0, 0)

    def mirrored(self, blocks, mirror):
        dot = functools.partial(jnp.dot, preferred_element_type=jnp.float32)

        def flip(values, which):
            top, low = halves(jnp.concatenate(values, axis=0))
            return dot(top, mirror[which]) + dot(low, mirror[which])

        flat = [part for k in range(self.outer) for pair in blocks[k] for part in pair]
        per = 2 * len(blocks[0])
        low = flip(flat[:per], 0)
        high = flip(flat[per:], 1)
        out = []
        for k in range(self.outer):
            part, base = (low, 0) if k == 0 else (high, (self.outer - k - 1) * per)
            take = lambda i: part[(base + i) * 8 : (base + i + 1) * 8]
            out.append([(take(2 * i), -take(2 * i + 1)) for i in range(per // 2)])
        return out

    def spread(self, first, second, strided, result):
        rows, fill = self.rows, TILE - 2 * self.rows
        for t in range(self.length // TILE):
            lanes = pl.ds(t * TILE, TILE)
            parts = [first[:, lanes], second[:, lanes]]
            if fill:
                parts.append(jnp.zeros((fill, TILE), jnp.float32))
            strided[pl.ds(t * TILE, TILE), :] = jnp.concatenate(parts, axis=0).T
        for k in range(self.outer):
            slab = strided[pl.ds(k, self.inner, stride=self.outer), :].T
            result[k] = slab[: 2 * rows, :]

    def collect(self, slabs, strided, results):
        rows = self.rows
        for k in range(self.outer):
            slab = slabs(k)
            fill = TILE - slab.shape[0]
            if fill:
                slab = jnp.concatenate([slab, jnp.zeros((fill, self.inner), jnp.float32)], axis=0)
            strided[pl.ds(k, self.inner, stride=self.outer), :] = slab.T
        for t in range(self.length // TILE):
            block = strided[pl.ds(t * TILE, TILE), :].T
            for i, result in enumerate(results):
                result[:, pl.ds(t * TILE, TILE)] = block[i * rows : (i + 1) * rows, :]


def signed_waves(position, count):
    signed = jnp.where(position < count // 2, position, position - count)
    waves = 4.0 * signed.astype(jnp.float32) / count
    return waves, jnp.where(position == count // 2, jnp.float32(0.0), waves)


def first_waves(piece, k):
    lanes = lax.broadcasted_iota(jnp.int32, (1, piece.inner), 1)
    return signed_waves(piece.outer * lanes + k, piece.length)


def inverse_denominator(wave_first, wave_second):
    square = wave_first * wave_first + wave_second * wave_second
    return 1.0 / (1.0 + time_step * (square * square - square))


def second_wave(piece, position):
    shape = (position.shape[0], piece.inner)
    return jnp.broadcast_to(signed_waves(position, piece.length)[0], shape)


def row_index(count, width):
    return lax.broadcasted_iota(jnp.int32, (count, width), 0)


def start_kernel(length, rows, field, target, twiddle, matrix, out, both_p, *scratch):
    piece = Pieces(length, rows, *scratch[:4])
    piece.spread(field, target, scratch[4], both_p)

    def body(r0):
        at = pl.ds(r0, piece.step)
        for k in range(piece.outer):
            piece.put(k, at, 0, both_p[k, at, :])

    piece.chunks(rows, body)
    piece.outgoing_kept(twiddle, matrix, out)


def slope_second_kernel(length, rows, field_p, twiddle, out_matrix, in_matrix, kept, result, *scratch):
    piece = Pieces(length, rows, *scratch)

    def body(r0):
        at = pl.ds(r0, piece.step)
        for k in range(piece.outer):
            piece.put(k, at, 0, field_p[k, at, :])

    piece.chunks(rows, body)
    for j in range(piece.outer):
        piece.clear_other(j)

    def write(r0, items):
        for j, (re, im) in enumerate(items):
            at, wide = piece.kept_lanes(j)
            base = at - j * piece.inner
            position = j * piece.inner + kept[:, base : base + wide]
            slope = 2.0 * signed_waves(position, length)[1]
            piece.turned[pl.ds(r0, piece.step), pl.ds(at, wide)] = -slope * im[:, base : base + wide]
            piece.turned[pl.ds(rows + r0, piece.step), pl.ds(at, wide)] = slope * re[:, base : base + wide]

    piece.outgoing(rows, -1.0, twiddle, out_matrix, True, write)
    piece.incoming(rows, 1.0, twiddle, in_matrix, real_out=True)
    result[...] = piece.z[:, :, : piece.inner]


def spread_kernel(length, rows, forcing, result, strided):
    Pieces(length, rows).spread(forcing.at[0], forcing.at[1], strided, result)


def collect_kernel(length, rows, slabs, result, strided):
    piece = Pieces(length, rows)
    piece.collect(lambda k: slabs[k], strided, [result.at[i] for i in range(result.shape[0])])


def weight_of(device, r0, step, inner):
    alone = (row_index(step, inner) + r0 + device) == 0
    return jnp.where(alone, jnp.float32(1.0), jnp.float32(2.0))


def slope_kernel(length, rows, device_ref, source, in_twiddle, in_matrix, out_twiddle, out_matrix, out, state, *scratch):
    device = device_ref[0]
    piece = Pieces(length, rows, *scratch)
    half = piece.half
    piece.turn_lines(source)
    piece.incoming(half, -1.0, in_twiddle, in_matrix)

    def body(r0):
        at, also = pl.ds(r0, piece.step), pl.ds(half + r0, piece.step)
        weight = weight_of(device, r0, piece.step, piece.inner)
        for k in range(piece.outer):
            re, im = piece.get(k, at, 0), piece.get(k, at, 1)
            state[k, at, :], state[k, also, :] = re, im
            scale = first_waves(piece, k)[1] * weight
            piece.put(k, at, 0, -scale * im)
            piece.put(k, at, 1, scale * re)

    piece.chunks(half, body)
    piece.outgoing(half, 1.0, out_twiddle, out_matrix, False, piece.write_full(out, False))


def total_kernel(length, rows, device_ref, source, coef, in_twiddle, in_matrix, out_twiddle, out_matrix, out, *scratch):
    device = device_ref[0]
    piece = Pieces(length, rows, *scratch)
    half = piece.half
    piece.turn_lines(source)
    piece.incoming(half, -1.0, in_twiddle, in_matrix)

    def body(r0):
        at, also = pl.ds(r0, piece.step), pl.ds(half + r0, piece.step)
        weight = weight_of(device, r0, piece.step, piece.inner)
        for k in range(piece.outer):
            re, im = piece.get(k, at, 0), piece.get(k, at, 1)
            deriv = first_waves(piece, k)[1]
            scale = 1.0 / time_step
            piece.put(k, at, 0, weight * (scale * coef[k, at, :] - deriv * im))
            piece.put(k, at, 1, weight * (scale * coef[k, also, :] + deriv * re))

    piece.chunks(half, body)
    piece.outgoing(half, 1.0, out_twiddle, out_matrix, False, piece.write_full(out, False))


def edge_inverses(piece, k):
    wave_first = first_waves(piece, k)[0]
    middle = jnp.full((1, 1), piece.length // 2, jnp.int32)
    zero = jnp.zeros((1, 1), jnp.int32)
    return [inverse_denominator(wave_first, signed_waves(p, piece.length)[0]) for p in (zero, middle)]


def next_kernel(length, rows, device_ref, source, state, forcing, in_twiddle, in_matrix, out_twiddle, out_matrix, mirror, out, *scratch):
    device = device_ref[0]
    piece = Pieces(length, rows, *scratch)
    half, step, inner = piece.half, piece.step, piece.inner
    late = device >= (length // rows) // 2
    piece.turn_lines(source)
    piece.incoming(half, -1.0, in_twiddle, in_matrix)

    def body(r0):
        at, also = pl.ds(r0, step), pl.ds(half + r0, step)
        index = row_index(step, 1) + r0
        low_wave = second_wave(piece, device * rows + index)
        high_wave = second_wave(piece, device * rows + half + index)
        moved = jnp.logical_and(row_index(step, inner) + r0 == 0, late)
        weight = weight_of(device, r0, step, inner)
        for k in range(piece.outer):
            wave_first = first_waves(piece, k)[0]
            low = inverse_denominator(wave_first, low_wave)
            high = inverse_denominator(wave_first, high_wave)
            for part in range(2):
                own = state[k, pl.ds(part * half + r0, step), :] + time_step * piece.get(k, at, part)
                own = weight * own
                f_low = time_step * forcing[k, pl.ds(part * rows + r0, step), :]
                f_high = time_step * forcing[k, pl.ds(part * rows + half + r0, step), :]
                piece.put(k, at, part, (f_low + jnp.where(moved, 0.0, own)) * low)
                piece.put(k, also, part, (f_high + jnp.where(moved, own, 0.0)) * high)

    piece.chunks(half, body)

    @pl.when(device == 0)
    def _():
        at = pl.ds(0, 8)
        blocks = []
        for k in range(piece.outer):
            own = tuple(
                state[k, pl.ds(part * half, 8), :] + time_step * piece.get(k, at, part) for part in range(2)
            )
            full = tuple(
                own[part] + time_step * forcing[k, pl.ds(part * rows, 8), :] for part in range(2)
            )
            blocks.append([own, full])
        flipped = piece.mirrored(blocks, mirror)
        rest = pl.ds(0, 16)
        row0 = row_index(16, inner) == 0
        for k in range(piece.outer):
            zero, middle = edge_inverses(piece, k)
            for part in range(2):
                own, full = blocks[k][0][part], blocks[k][1][part]
                own_c, full_c = flipped[k][0][part], flipped[k][1][part]
                value = 0.5 * ((full + full_c) * zero + (own - own_c) * middle)
                replace(piece, k, part, value)

    piece.outgoing(rows, 1.0, out_twiddle, out_matrix, False, piece.write_full(out, False))


def replace(piece, k, part, value):
    lanes = pl.ds(part * piece.inner, piece.inner)
    row0 = row_index(16, piece.inner) == 0
    value = jnp.concatenate([value, value], axis=0)
    for held, new in zip((piece.top, piece.low), halves(value)):
        old = held[k, pl.ds(0, 16), lanes].astype(jnp.float32)
        held[k, pl.ds(0, 16), lanes] = jnp.where(row0, new.astype(jnp.float32), old).astype(jnp.bfloat16)


def misfit_kernel(length, rows, device_ref, source, in_twiddle, in_matrix, out_twiddle, out_matrix, mirror, out, full, coef, total_out, *scratch):
    device = device_ref[0]
    piece = Pieces(length, rows, *scratch)
    half, step, inner = piece.half, piece.step, piece.inner
    late = device >= (length // rows) // 2
    piece.turn_full(source)
    piece.incoming(rows, -1.0, in_twiddle, in_matrix)

    def body(r0):
        at, also = pl.ds(r0, step), pl.ds(half + r0, step)
        index = row_index(step, 1) + r0
        low_wave = second_wave(piece, device * rows + index)
        high_wave = second_wave(piece, device * rows + half + index)
        moved = jnp.logical_and(row_index(step, inner) + r0 == 0, late)
        weight = weight_of(device, r0, step, inner)
        for k in range(piece.outer):
            wave_first = first_waves(piece, k)[0]
            low = time_step * inverse_denominator(wave_first, low_wave)
            high = time_step * inverse_denominator(wave_first, high_wave)
            for part in range(2):
                low_value = piece.get(k, at, part) * low
                high_value = piece.get(k, also, part) * high
                full[k, pl.ds(part * rows + r0, step), :] = low_value
                full[k, pl.ds(part * rows + half + r0, step), :] = high_value
                own = jnp.where(moved, high_value, low_value)
                coef[k, pl.ds(part * half + r0, step), :] = own
                piece.put(k, at, part, weight * own)

    piece.chunks(half, body)

    @pl.when(device == 0)
    def _():
        at = pl.ds(0, 8)
        blocks = [[(piece.get(k, at, 0), piece.get(k, at, 1))] for k in range(piece.outer)]
        flipped = piece.mirrored(blocks, mirror)
        row0 = row_index(8, inner) == 0
        for k in range(piece.outer):
            zero, middle = edge_inverses(piece, k)
            for part in range(2):
                own, own_c = blocks[k][0][part], flipped[k][0][part]
                first = (0.5 * time_step) * (own + own_c) * zero
                value = first + (0.5 * time_step) * (own - own_c) * middle
                at_full, at_coef = pl.ds(part * rows, 8), pl.ds(part * half, 8)
                full[k, at_full, :] = jnp.where(row0, first, full[k, at_full, :])
                coef[k, at_coef, :] = jnp.where(row0, value, coef[k, at_coef, :])
                replace(piece, k, part, value)

    piece.outgoing(half, 1.0, out_twiddle, out_matrix, False, piece.write_full(out, False))
    total_out[...] = jnp.sum(source[:, pl.ds(rows, 8), :], axis=0)


def nonlinear_kernel(length, rows, source, second, twiddle, in_matrix, out_matrix, out, first_out, *scratch):
    piece = Pieces(length, rows, *scratch)
    piece.turn_kept(source)
    piece.unpack_middle()
    piece.incoming(rows, 1.0, twiddle, in_matrix, real_out=True)

    def body(r0):
        at = pl.ds(r0, piece.step)
        for k in range(piece.outer):
            first, other = piece.get(k, at, 0), second[k, at, :]
            first_out[k, at, :] = first
            piece.put(k, at, 0, -0.5 * (first * first + other * other))

    piece.chunks(rows, body)
    piece.outgoing_kept(twiddle, out_matrix, out)


def joint_kernel(length, rows, source, first, second, twiddle, in_matrix, out_matrix, out, second_out, *scratch):
    piece = Pieces(length, rows, *scratch)
    piece.turn_kept(source)
    piece.unpack_middle()
    piece.incoming(rows, 1.0, twiddle, in_matrix, real_out=True)

    def body(r0):
        at = pl.ds(r0, piece.step)
        for k in range(piece.outer):
            value = piece.get(k, at, 0)
            second_out[k, at, :] = value * second[k, at, :]
            piece.put(k, at, 0, value * first[k, at, :])

    piece.chunks(rows, body)
    piece.outgoing_kept(twiddle, out_matrix, out)


def residual_kernel(length, rows, source, both_p, twiddle, in_matrix, out_matrix, out, field_out, *scratch):
    piece = Pieces(length, rows, *scratch[:4])
    strided, total = scratch[4:]
    piece.turn_full(source)
    piece.unpack_middle()
    piece.incoming(rows, 1.0, twiddle, in_matrix, real_out=True)
    piece.collect(lambda k: piece.get(k, pl.ds(0, rows), 0), strided, [field_out])
    total[...] = jnp.zeros_like(total)

    def body(r0):
        at = pl.ds(r0, piece.step)
        for k in range(piece.outer):
            residual = piece.get(k, at, 0) - both_p[k, pl.ds(rows + r0, piece.step), :]
            total[...] += residual * residual
            piece.put(k, at, 0, residual)

    piece.chunks(rows, body)
    piece.outgoing(rows, -1.0, twiddle, out_matrix, True, piece.write_full(out, True))
    value = 0.5 * jnp.sum(total[...])
    out[:, pl.ds(rows, 8), :] = jnp.full((out.shape[0], 8, 2 * rows), value, jnp.float32)


def last_kernel(length, rows, source, second, twiddle, in_matrix, field_out, *scratch):
    piece = Pieces(length, rows, *scratch[:4])
    piece.turn_kept(source)
    piece.unpack_middle()
    piece.incoming(rows, 1.0, twiddle, in_matrix, real_out=True)
    piece.collect(
        lambda k: piece.get(k, pl.ds(0, rows), 0) + second[k], scratch[4], [field_out]
    )


def member_step(device, field, target, forcing_p, devices, rows, length):
    outer, inner = split_length(length)
    half = rows // 2
    float32 = jnp.float32
    shape = lambda *dims: jax.ShapeDtypeStruct(dims, float32)
    kept_blocks = shape(devices, rows * rows // TILE, TILE)
    half_blocks = shape(devices, half, 2 * rows)
    blocks = shape(devices, rows, 2 * rows)
    longer = shape(devices, rows + 8, 2 * rows)
    pair, one = shape(outer, 2 * rows, inner), shape(outer, rows, inner)
    plain = shape(rows, length)
    step = math.gcd(half, 16)
    base = [
        pltpu.VMEM((2 * rows, length), float32),
        pltpu.VMEM((outer, rows, 2 * inner), jnp.bfloat16),
        pltpu.VMEM((outer, rows, 2 * inner), jnp.bfloat16),
        pltpu.VMEM((outer, rows, 2 * inner), float32),
    ]
    strided = pltpu.VMEM((length, TILE), float32)
    total = pltpu.VMEM((step, inner), float32)
    vmem = pl.BlockSpec(memory_space=pltpu.VMEM)
    smem = pl.BlockSpec(memory_space=pltpu.SMEM)

    natural, kept, lines = orders(length, rows)
    tw_natural, tw_kept, tw_lines = [jnp.asarray(twiddle_table(length, o)) for o in (natural, kept, lines)]
    matrix = lambda *args: jnp.asarray(matrix_table(length, *args))
    forward, backward = matrix(-1.0, natural, natural), matrix(1.0, natural, natural)
    kept_out, kept_in = matrix(-1.0, natural, kept), matrix(1.0, kept, natural)
    lines_in = matrix(-1.0, lines, natural)
    mirror = jnp.asarray(mirror_table(length))
    kept_lane = jnp.asarray(kept[None, :].astype(np.int32))

    def call(body, outs, scratch, *operands):
        return pl.pallas_call(
            functools.partial(body, length, rows),
            out_shape=outs,
            in_specs=[smem if operand is device else vmem for operand in operands],
            out_specs=jax.tree.map(lambda leaf: vmem, outs),
            scratch_shapes=scratch,
            compiler_params=pltpu.CompilerParams(vmem_limit_bytes=48 * 2**20),
            cost_estimate=pl.CostEstimate(flops=6 * 10**9, bytes_accessed=4 * 2**20, transcendentals=0),
        )(*operands)

    def move(value):
        return lax.all_to_all(value, axes, split_axis=0, concat_axis=0, tiled=True)

    spectral_tables = (tw_lines, lines_in, tw_natural, backward)
    slope_tables = (tw_kept, kept_out, kept_in, kept_lane)
    sent, both_p = call(start_kernel, (kept_blocks, pair), base + [strided], field, target, tw_kept, kept_out)
    second = call(slope_second_kernel, one, base, both_p, *slope_tables)
    sent, state = call(slope_kernel, (half_blocks, one), base, device, move(sent), *spectral_tables)
    sent, first = call(nonlinear_kernel, (kept_blocks, one), base, move(sent), second, tw_kept, kept_in, kept_out)
    sent = call(next_kernel, blocks, base, device, move(sent), state, forcing_p, *spectral_tables, mirror)
    sent, next_field = call(
        residual_kernel, (longer, plain), base + [strided, total],
        move(sent), both_p, tw_natural, backward, forward,
    )
    sent, full, coef, sums = call(
        misfit_kernel, (half_blocks, pair, one, shape(8, 2 * rows)), base,
        device, move(sent), tw_natural, forward, tw_natural, backward, mirror,
    )
    sent, product = call(
        joint_kernel, (kept_blocks, one), base, move(sent), first, second, tw_kept, kept_in, kept_out
    )
    second_part = call(slope_second_kernel, one, base, product, *slope_tables)
    sent = call(total_kernel, half_blocks, base, device, move(sent), coef, *spectral_tables)
    field_grad = call(last_kernel, plain, base + [strided], move(sent), second_part, tw_kept, kept_in)
    return next_field, sums[0, 0], field_grad, full


def per_device(devices, initial_field, target_field, forcing):
    members, rows, length = initial_field.shape
    device = lax.axis_index(axes).astype(jnp.int32).reshape(1)
    outer, inner = split_length(length)
    vmem = pl.BlockSpec(memory_space=pltpu.VMEM)
    strided = pltpu.VMEM((length, TILE), jnp.float32)

    def reorder(body, shape, operand):
        return pl.pallas_call(
            functools.partial(body, length, rows),
            out_shape=jax.ShapeDtypeStruct(shape, jnp.float32),
            in_specs=[vmem],
            out_specs=vmem,
            scratch_shapes=[strided],
        )(operand)

    forcing_p = reorder(spread_kernel, (outer, 2 * rows, inner), forcing)
    results = [
        member_step(device, initial_field[m], target_field[m], forcing_p, devices, rows, length)
        for m in range(members)
    ]
    next_field = jnp.stack([one[0] for one in results])
    objective = sum(one[1] for one in results) / (members * length * length)
    field_grad = jnp.stack([one[2] for one in results])
    forcing_grad = reorder(collect_kernel, (2, rows, length), sum(one[3] for one in results))
    return (next_field, objective, field_grad, forcing_grad)


def solution(mesh):
    devices = mesh.shape["px"] * mesh.shape["py"]
    spec = P(None, axes, None)
    return jax.shard_map(
        functools.partial(per_device, devices),
        mesh=mesh,
        in_specs=(spec, spec, spec),
        out_specs=(spec, P(), spec, spec),
        check_vma=False,
    )
```

time: 291 us -> 225 us (0.77)
  blocking collectives: 151 us -> 98.4 us
  waiting for transfers between devices: 71.6 us -> 47.1 us
  local copies, waits for them, and re-layouts: 11.1 us -> 18.3 us
    all_to_all x5 -> x4, blocking collectives: 151 us -> 98.4 us  [move(): return lax.all_to_all(value, axes, split_axis=0, concat_axis=0, tiled=True)]
    all_to_all x3 -> x4, waiting for transfers between devices: 71.6 us -> 47.1 us  [move(): return lax.all_to_all(value, axes, split_axis=0, concat_axis=0, tiled=True)]
    unnamed x32 -> x60, local copies, waits for them, and re-layouts: 10.6 us -> 17.8 us
    pallas_call x9 -> x11, Pallas kernels: 33.4 us -> 35.9 us  [call(): pl.pallas_call(functools.partial(body, length, rows), out_shape=outs, in_...]
    all_to_all x3 -> x4, starting transfers between devices: 14.6 us -> 16.2 us  [move(): return lax.all_to_all(value, axes, split_axis=0, concat_axis=0, tiled=True)]
  transfers between devices with their start and end apart: 3 -> 4, of which waited for: 3 -> 4; matrix products, arithmetic and copies ran while one was open for 0% -> 0% of each run, Pallas kernels for 2% -> 5%
where the time goes in v2:
time: 225 us; the launch traced here: 224 us
  blocking collectives  98.4 us (44%)
  waiting for transfers between devices  47.1 us (21%)
  Pallas kernels  41.7 us (19%)
  local copies, waits for them, and re-layouts  18.3 us (8%)
  starting transfers between devices  16.2 us (7%)
  between operations  2.61 us (1%)
    all_to_all x4, blocking collectives, move(): return lax.all_to_all(value, axes, split_axis=0, concat_axis=0, tiled=True)  98.4 us
    all_to_all x4, waiting for transfers between devices, move(): return lax.all_to_all(value, axes, split_axis=0, concat_axis=0, tiled=True)  47.1 us
    pallas_call x11, Pallas kernels, call(): pl.pallas_call(functools.partial(body, length, rows), out_shape=outs, in_...  35.9 us
    unnamed x60, local copies, waits for them, and re-layouts  17.8 us
    all_to_all x4, starting transfers between devices, move(): return lax.all_to_all(value, axes, split_axis=0, concat_axis=0, tiled=True)  16.2 us
    pallas_call x2, Pallas kernels, reorder(): pl.pallas_call(functools.partial(body, length, rows), out_shape=jax.Shape...  5.79 us
  transfers between devices with their start and end apart: 4, of which 4 were waited for; matrix products, arithmetic and copies ran while one was open for 0% of the time, Pallas kernels for 5%

profile of v2, /device:TPU:0, one launch (start us, length us, event | category | flops | bytes accessed | tf_op | source)
XLA Modules:
  0.0 224.4 jit_solution(9545146352683609547)
XLA Ops:
  4.7 2.9 %shard_map.156 = (f32[32,32,128]{2,1,0:T(8,128)}, f32[8,128,256]{2,1,0:T(8,128)S(1)}) custom-call(f32[64,2048]{1,0:T(8,128)S(1)} %bitcast.6, f32[64,2048]{1,0:T(8,128)S(1)} %bitcast.7, f32[2,8,256]{2,1,0:T(8,128)S(1)} %copy-done.15, bf16[2,512,512]{2,1,0:T(8,128)(2,1)S(1)} %copy-done.5), custom_call_target="tpu_custom_call" | custom-call | flops 6000000000 | bytes 4194304 | tf_op jit(solution)/shard_map/pallas_call | solution.py:641
  8.5 7.3 %all-to-all-start = ((f32[32,32,128]{2,1,0:T(8,128)}), f32[32,32,128]{2,1,0:T(8,128)S(1)}, u32[]{:S(2)}, u32[]{:S(2)}) async-start(f32[32,32,128]{2,1,0:T(8,128)} %get-tuple-element.18), calls=%async_computation | async-start | bytes 1048576 | tf_op jit(solution)/shard_map/all_to_all | solution.py:652
  15.8 15.6 %all-to-all-done.source = f32[32,32,128]{2,1,0:T(8,128)S(1)} async-done(((f32[32,32,128]{2,1,0:T(8,128)}), f32[32,32,128]{2,1,0:T(8,128)S(1)}, u32[]{:S(2)}, u32[]{:S(2)}) %all-to-all-start) | async-done | bytes 524320 | tf_op jit(solution)/shard_map/all_to_all | solution.py:652
  33.9 2.9 %shard_map.157 = (f32[32,32,128]{2,1,0:T(8,128)}, f32[8,64,256]{2,1,0:T(8,128)S(1)}) custom-call(s32[1]{0:T(128)} %bitcast.device_ref, f32[32,32,128]{2,1,0:T(8,128)S(1)} %all-to-all-done.source, f32[2,8,256]{2,1,0:T(8,128)S(1)} %copy-done.18, bf16[2,512,512]{2,1,0:T(8,128)(2,1)S(1)} %copy-done.10, f32[2,8,256]{2,1,0:T(8,128)S(1)} %copy-done.17, ...), custom_call_target="tpu_custom_call" | custom-call | flops 6000000000 | bytes 4194304 | tf_op jit(solution)/shard_map/pallas_call | solution.py:641
  36.8 3.0 %all-to-all-start.1 = ((f32[32,32,128]{2,1,0:T(8,128)}), f32[32,32,128]{2,1,0:T(8,128)S(1)}, u32[]{:S(2)}, u32[]{:S(2)}) async-start(f32[32,32,128]{2,1,0:T(8,128)} %get-tuple-element.19), calls=%async_computation.1 | async-start | bytes 1048576 | tf_op jit(solution)/shard_map/all_to_all | solution.py:652
  41.0 2.7 %shard_map.158.second = f32[8,64,256]{2,1,0:T(8,128)S(1)} custom-call(f32[8,128,256]{2,1,0:T(8,128)S(1)} %copy-done.21, f32[2,8,256]{2,1,0:T(8,128)S(1)} %copy-done.16, bf16[2,512,512]{2,1,0:T(8,128)(2,1)S(1)} %copy-done.6, bf16[2,512,512]{2,1,0:T(8,128)(2,1)S(1)} %copy-done.4, s32[1,256]{1,0:T(1,128)S(1)} %copy-done.19), custom_call_target="tpu_custom_call" | custom-call | flops 6000000000 | bytes 4194304 | tf_op jit(solution)/shard_map/pallas_call | solution.py:641
  44.6 10.8 %all-to-all-done.1.source = f32[32,32,128]{2,1,0:T(8,128)S(1)} async-done(((f32[32,32,128]{2,1,0:T(8,128)}), f32[32,32,128]{2,1,0:T(8,128)S(1)}, u32[]{:S(2)}, u32[]{:S(2)}) %all-to-all-start.1) | async-done | bytes 524320 | tf_op jit(solution)/shard_map/all_to_all | solution.py:652
  56.4 4.2 %shard_map.159 = (f32[32,32,128]{2,1,0:T(8,128)}, f32[8,64,256]{2,1,0:T(8,128)S(1)}) custom-call(f32[32,32,128]{2,1,0:T(8,128)S(1)} %all-to-all-done.1.source, f32[8,64,256]{2,1,0:T(8,128)S(1)} %copy-done.24, f32[2,8,256]{2,1,0:T(8,128)S(1)} %copy-done.16, bf16[2,512,512]{2,1,0:T(8,128)(2,1)S(1)} %copy-done.4, bf16[2,512,512]{2,1,0:T(8,128)(2,1)S(1)} %copy-done.6), custom_call_target="tpu_custom_call" | custom-call | flops 6000000000 | bytes 4194304 | tf_op jit(solution)/shard_map/pallas_call | solution.py:641
  61.5 3.0 %all-to-all-start.2 = ((f32[32,32,128]{2,1,0:T(8,128)}), f32[32,32,128]{2,1,0:T(8,128)S(1)}, u32[]{:S(2)}, u32[]{:S(2)}) async-start(f32[32,32,128]{2,1,0:T(8,128)} %get-tuple-element.21), calls=%async_computation.2 | async-start | bytes 1048576 | tf_op jit(solution)/shard_map/all_to_all | solution.py:652
  64.5 2.9 %shard_map.160.forcing = f32[8,128,256]{2,1,0:T(8,128)} custom-call(f32[2,64,2048]{2,1,0:T(8,128)} %forcing.1), custom_call_target="tpu_custom_call" | custom-call | tf_op jit(solution)/shard_map/pallas_call | solution.py:686
  67.4 12.7 %all-to-all-done.2.source = f32[32,32,128]{2,1,0:T(8,128)S(1)} async-done(((f32[32,32,128]{2,1,0:T(8,128)}), f32[32,32,128]{2,1,0:T(8,128)S(1)}, u32[]{:S(2)}, u32[]{:S(2)}) %all-to-all-start.2) | async-done | bytes 524320 | tf_op jit(solution)/shard_map/all_to_all | solution.py:652
  83.7 3.4 %shard_map.161 = f32[32,64,128]{2,1,0:T(8,128)S(1)} custom-call(s32[1]{0:T(128)} %bitcast.device_ref, f32[32,32,128]{2,1,0:T(8,128)S(1)} %all-to-all-done.2.source, f32[8,64,256]{2,1,0:T(8,128)S(1)} %get-tuple-element.22.state, f32[8,128,256]{2,1,0:T(8,128)S(1)} %copy-done.1, f32[2,8,256]{2,1,0:T(8,128)S(1)} %copy-done.18, ...), custom_call_target="tpu_custom_call" | custom-call | flops 6000000000 | bytes 4194304 | tf_op jit(solution)/shard_map/pallas_call | solution.py:641
  87.2 28.7 %all_to_all.40.source = f32[32,64,128]{2,1,0:T(8,128)S(1)} all-to-all(f32[32,64,128]{2,1,0:T(8,128)S(1)} %shard_map.161), channel_id=1, replica_groups=mesh['px'=8,'py'=4] {'px','py'}, dimensions={0} | all-to-all | bytes 2097152 | tf_op jit(solution)/shard_map/all_to_all | solution.py:652
  115.9 4.7 %shard_map.162 = (f32[32,72,128]{2,1,0:T(8,128)S(1)}, f32[64,2048]{1,0:T(8,128)}) custom-call(f32[32,64,128]{2,1,0:T(8,128)S(1)} %all_to_all.40.source, f32[8,128,256]{2,1,0:T(8,128)S(1)} %copy-done.22, f32[2,8,256]{2,1,0:T(8,128)S(1)} %copy-done.17, bf16[2,512,512]{2,1,0:T(8,128)(2,1)S(1)} %copy-done.9, bf16[2,512,512]{2,1,0:T(8,128)(2,1)S(1)} %copy-done.13), custom_call_target="tpu_custom_call" | custom-call | flops 6000000000 | bytes 4194304 | tf_op jit(solution)/shard_map/pallas_call | solution.py:641
  120.6 34.0 %all_to_all.41.source = f32[32,72,128]{2,1,0:T(8,128)S(1)} all-to-all(f32[32,72,128]{2,1,0:T(8,128)S(1)} %get-tuple-element.24), channel_id=1, replica_groups=mesh['px'=8,'py'=4] {'px','py'}, dimensions={0} | all-to-all | bytes 2359296 | tf_op jit(solution)/shard_map/all_to_all | solution.py:652
  154.7 3.5 %shard_map.163 = (f32[32,32,128]{2,1,0:T(8,128)S(1)}, f32[8,128,256]{2,1,0:T(8,128)S(1)}, f32[8,64,256]{2,1,0:T(8,128)S(1)}, f32[8,128]{1,0:T(8,128)S(1)}) custom-call(s32[1]{0:T(128)} %bitcast.device_ref, f32[32,72,128]{2,1,0:T(8,128)S(1)} %all_to_all.41.source, f32[2,8,256]{2,1,0:T(8,128)S(1)} %copy-done.17, bf16[2,512,512]{2,1,0:T(8,128)(2,1)S(1)} %copy-done.13, ...), custom_call_target="tpu_custom_call" | custom-call | flops 6000000000 | bytes 4194304 | tf_op jit(solution)/shard_map/pallas_call | solution.py:641
  159.1 17.3 %all_to_all.42.source = f32[32,32,128]{2,1,0:T(8,128)S(1)} all-to-all(f32[32,32,128]{2,1,0:T(8,128)S(1)} %get-tuple-element.26), channel_id=1, replica_groups=mesh['px'=8,'py'=4] {'px','py'}, dimensions={0} | all-to-all | bytes 1048576 | tf_op jit(solution)/shard_map/all_to_all | solution.py:652
  176.5 3.5 %shard_map.164 = (f32[32,32,128]{2,1,0:T(8,128)S(1)}, f32[8,64,256]{2,1,0:T(8,128)S(1)}) custom-call(f32[32,32,128]{2,1,0:T(8,128)S(1)} %all_to_all.42.source, f32[8,64,256]{2,1,0:T(8,128)S(1)} %copy-done.27, f32[8,64,256]{2,1,0:T(8,128)S(1)} %copy-done.25, f32[2,8,256]{2,1,0:T(8,128)S(1)} %copy-done.16, bf16[2,512,512]{2,1,0:T(8,128)(2,1)S(1)} %copy-done.4, ...), custom_call_target="tpu_custom_call" | custom-call | flops 6000000000 | bytes 4194304 | tf_op jit(solution)/shard_map/pallas_call | solution.py:641
  179.9 18.3 %all_to_all.43.source = f32[32,32,128]{2,1,0:T(8,128)S(1)} all-to-all(f32[32,32,128]{2,1,0:T(8,128)S(1)} %get-tuple-element.28), channel_id=1, replica_groups=mesh['px'=8,'py'=4] {'px','py'}, dimensions={0} | all-to-all | bytes 1048576 | tf_op jit(solution)/shard_map/all_to_all | solution.py:652
  198.2 2.9 %shard_map.165 = f32[32,32,128]{2,1,0:T(8,128)} custom-call(s32[1]{0:T(128)} %bitcast.device_ref, f32[32,32,128]{2,1,0:T(8,128)S(1)} %all_to_all.43.source, f32[8,64,256]{2,1,0:T(8,128)S(1)} %get-tuple-element.29.coef, f32[2,8,256]{2,1,0:T(8,128)S(1)} %copy-done.18, bf16[2,512,512]{2,1,0:T(8,128)(2,1)S(1)} %copy-done.12, f32[2,8,256]{2,1,0:T(8,128)S(1)} %copy-done.17, ...), custom_call_target="tpu_custom_call" | custom-call | flops 6000000000 | bytes 4194304 | tf_op jit(solution)/shard_map/pallas_call | solution.py:641
  201.1 3.0 %all-to-all-start.7 = ((f32[32,32,128]{2,1,0:T(8,128)}), f32[32,32,128]{2,1,0:T(8,128)S(1)}, u32[]{:S(2)}, u32[]{:S(2)}) async-start(f32[32,32,128]{2,1,0:T(8,128)} %shard_map.165), calls=%async_computation.7 | async-start | bytes 1048576 | tf_op jit(solution)/shard_map/all_to_all | solution.py:652
  204.6 2.9 %shard_map.168 = f32[2,64,2048]{2,1,0:T(8,128)} custom-call(f32[8,128,256]{2,1,0:T(8,128)} %copy-done), custom_call_target="tpu_custom_call" | custom-call | tf_op jit(solution)/shard_map/pallas_call | solution.py:686
  208.1 2.8 %shard_map.166.second = f32[8,64,256]{2,1,0:T(8,128)S(1)} custom-call(f32[8,64,256]{2,1,0:T(8,128)S(1)} %get-tuple-element.30.field_p, f32[2,8,256]{2,1,0:T(8,128)S(1)} %copy-done.16, bf16[2,512,512]{2,1,0:T(8,128)(2,1)S(1)} %copy-done.6, bf16[2,512,512]{2,1,0:T(8,128)(2,1)S(1)} %copy-done.4, s32[1,256]{1,0:T(1,128)S(1)} %copy-done.19), custom_call_target="tpu_custom_call" | custom-call | flops 6000000000 | bytes 4194304 | tf_op jit(solution)/shard_map/pallas_call | solution.py:641
  211.7 8.0 %all-to-all-done.7.source = f32[32,32,128]{2,1,0:T(8,128)S(1)} async-done(((f32[32,32,128]{2,1,0:T(8,128)}), f32[32,32,128]{2,1,0:T(8,128)S(1)}, u32[]{:S(2)}, u32[]{:S(2)}) %all-to-all-start.7) | async-done | bytes 524320 | tf_op jit(solution)/shard_map/all_to_all | solution.py:652
  (62 shorter events, 20.9 us)
Async XLA Ops:
  2.7 1.2 copy-start.5
  4.7 26.8 %copy-start.17 = (f32[2,8,256]{2,1,0:T(8,128)S(1)}, f32[2,8,256]{2,1,0:T(8,128)}, u32[]{:S(2)}) copy-start(f32[2,8,256]{2,1,0:T(8,128)} %constant.35.clone.out_twiddle.twiddle.in_twiddle) | copy-start | bytes 49156
  4.7 26.8 %copy-start.18 = (f32[2,8,256]{2,1,0:T(8,128)S(1)}, f32[2,8,256]{2,1,0:T(8,128)}, u32[]{:S(2)}) copy-start(f32[2,8,256]{2,1,0:T(8,128)} %constant.37.clone.in_twiddle) | copy-start | bytes 49156
  8.5 22.9 %all-to-all-start = ((f32[32,32,128]{2,1,0:T(8,128)}), f32[32,32,128]{2,1,0:T(8,128)S(1)}, u32[]{:S(2)}, u32[]{:S(2)}) async-start(f32[32,32,128]{2,1,0:T(8,128)} %get-tuple-element.18), calls=%async_computation | async-start | bytes 1048576 | tf_op jit(solution)/shard_map/all_to_all | solution.py:652
  31.5 1.2 copy-start.7
  32.7 1.2 copy-start.10
  33.9 5.9 %copy-start.4 = (bf16[2,512,512]{2,1,0:T(8,128)(2,1)S(1)}, bf16[2,512,512]{2,1,0:T(8,128)(2,1)}, u32[]{:S(2)}) copy-start(bf16[2,512,512]{2,1,0:T(8,128)(2,1)} %constant.41.clone.in_matrix) | copy-start | bytes 3145732
  33.9 5.9 %copy-start.6 = (bf16[2,512,512]{2,1,0:T(8,128)(2,1)S(1)}, bf16[2,512,512]{2,1,0:T(8,128)(2,1)}, u32[]{:S(2)}) copy-start(bf16[2,512,512]{2,1,0:T(8,128)(2,1)} %constant.40.clone.matrix.out_matrix) | copy-start | bytes 3145732
  33.9 5.9 %copy-start.16 = (f32[2,8,256]{2,1,0:T(8,128)S(1)}, f32[2,8,256]{2,1,0:T(8,128)}, u32[]{:S(2)}) copy-start(f32[2,8,256]{2,1,0:T(8,128)} %constant.36.clone.twiddle) | copy-start | bytes 49156
  33.9 5.9 %copy-start.19 = (s32[1,256]{1,0:T(1,128)S(1)}, s32[1,256]{1,0:T(1,128)}, u32[]{:S(2)}) copy-start(s32[1,256]{1,0:T(1,128)} %constant.44.clone.kept) | copy-start | bytes 3076
  36.8 18.6 %all-to-all-start.1 = ((f32[32,32,128]{2,1,0:T(8,128)}), f32[32,32,128]{2,1,0:T(8,128)S(1)}, u32[]{:S(2)}, u32[]{:S(2)}) async-start(f32[32,32,128]{2,1,0:T(8,128)} %get-tuple-element.19), calls=%async_computation.1 | async-start | bytes 1048576 | tf_op jit(solution)/shard_map/all_to_all | solution.py:652
  39.8 1.2 copy-start.21
  61.5 18.6 %all-to-all-start.2 = ((f32[32,32,128]{2,1,0:T(8,128)}), f32[32,32,128]{2,1,0:T(8,128)S(1)}, u32[]{:S(2)}, u32[]{:S(2)}) async-start(f32[32,32,128]{2,1,0:T(8,128)} %get-tuple-element.21), calls=%async_computation.2 | async-start | bytes 1048576 | tf_op jit(solution)/shard_map/all_to_all | solution.py:652
  64.4 15.6 %copy-start.14 = (bf16[2,256,256]{2,1,0:T(8,128)(2,1)S(1)}, bf16[2,256,256]{2,1,0:T(8,128)(2,1)}, u32[]{:S(2)}) copy-start(bf16[2,256,256]{2,1,0:T(8,128)(2,1)} %constant.43.clone.mirror) | copy-start | bytes 786436
  80.1 1.2 copy-start.1
  81.3 1.2 copy-start.8
  82.5 1.2 copy-start.11
  83.7 32.2 %copy-start.22 = (f32[8,128,256]{2,1,0:T(8,128)S(1)}, f32[8,128,256]{2,1,0:T(8,128)}, u32[]{:S(2)}) copy-start(f32[8,128,256]{2,1,0:T(8,128)} %copy-done.20) | copy-start | bytes 3145732
  87.2 28.7 %copy-start.9 = (bf16[2,512,512]{2,1,0:T(8,128)(2,1)S(1)}, bf16[2,512,512]{2,1,0:T(8,128)(2,1)}, u32[]{:S(2)}) copy-start(bf16[2,512,512]{2,1,0:T(8,128)(2,1)} %constant.39.clone.out_matrix.in_matrix) | copy-start | bytes 3145732
  87.2 28.7 %copy-start.13 = (bf16[2,512,512]{2,1,0:T(8,128)(2,1)S(1)}, bf16[2,512,512]{2,1,0:T(8,128)(2,1)}, u32[]{:S(2)}) copy-start(bf16[2,512,512]{2,1,0:T(8,128)(2,1)} %constant.38.clone.out_matrix.in_matrix) | copy-start | bytes 3145732
  154.7 21.8 %copy-start.25 = (f32[8,64,256]{2,1,0:T(8,128)S(1)}, f32[8,64,256]{2,1,0:T(8,128)}, u32[]{:S(2)}) copy-start(f32[8,64,256]{2,1,0:T(8,128)} %copy-done.23) | copy-start | bytes 1572868
  154.7 21.8 %copy-start.27 = (f32[8,64,256]{2,1,0:T(8,128)S(1)}, f32[8,64,256]{2,1,0:T(8,128)}, u32[]{:S(2)}) copy-start(f32[8,64,256]{2,1,0:T(8,128)} %copy-done.26) | copy-start | bytes 1572868
  176.5 21.8 %copy-start.12 = (bf16[2,512,512]{2,1,0:T(8,128)(2,1)S(1)}, bf16[2,512,512]{2,1,0:T(8,128)(2,1)}, u32[]{:S(2)}) copy-start(bf16[2,512,512]{2,1,0:T(8,128)(2,1)} %constant.42.clone.in_matrix) | copy-start | bytes 3145732
  201.1 18.6 %all-to-all-start.7 = ((f32[32,32,128]{2,1,0:T(8,128)}), f32[32,32,128]{2,1,0:T(8,128)S(1)}, u32[]{:S(2)}, u32[]{:S(2)}) async-start(f32[32,32,128]{2,1,0:T(8,128)} %shard_map.165), calls=%async_computation.7 | async-start | bytes 1048576 | tf_op jit(solution)/shard_map/all_to_all | solution.py:652
  (10 other events, 9.2 us)

commit v3 on v2

--- a/solution.py
+++ b/solution.py
@@ -630,9 +630,9 @@
 
     natural, kept, lines = orders(length, rows)
     tw_natural, tw_kept, tw_lines = [jnp.asarray(twiddle_table(length, o)) for o in (natural, kept, lines)]
-    matrix = lambda *args: jnp.asarray(matrix_table(length, *args))
+    matrix = lambda *args: matrix_table(length, *args)
     forward, backward = matrix(-1.0, natural, natural), matrix(1.0, natural, natural)
-    kept_out, kept_in = matrix(-1.0, natural, kept), matrix(1.0, kept, natural)
+    kept_out, kept_in = matrix(-1.0, natural, kept)[:, :inner], matrix(1.0, kept, natural)[:, :, :inner]
     lines_in = matrix(-1.0, lines, natural)
     mirror = jnp.asarray(mirror_table(length))
     kept_lane = jnp.asarray(kept[None, :].astype(np.int32))
@@ -644,7 +644,7 @@
             in_specs=[smem if operand is device else vmem for operand in operands],
             out_specs=jax.tree.map(lambda leaf: vmem, outs),
             scratch_shapes=scratch,
-            compiler_params=pltpu.CompilerParams(vmem_limit_bytes=48 * 2**20),
+            compiler_params=pltpu.CompilerParams(vmem_limit_bytes=20 * 2**20),
             cost_estimate=pl.CostEstimate(flops=6 * 10**9, bytes_accessed=4 * 2**20, transcendentals=0),
         )(*operands)
 

time: 225 us -> 221 us (0.982)
  local copies, waits for them, and re-layouts: 18.3 us -> 14.4 us
    unnamed x60 -> x62, local copies, waits for them, and re-layouts: 17.8 us -> 13.9 us
where the time goes in v3:
time: 221 us; the launch traced here: 220 us
  blocking collectives  98.4 us (45%)
  waiting for transfers between devices  46.8 us (21%)
  Pallas kernels  41.7 us (19%)
  starting transfers between devices  16.2 us (7%)
  local copies, waits for them, and re-layouts  14.4 us (7%)
  between operations  2.67 us (1%)
    all_to_all x4, blocking collectives, move(): return lax.all_to_all(value, axes, split_axis=0, concat_axis=0, tiled=True)  98.4 us
    all_to_all x4, waiting for transfers between devices, move(): return lax.all_to_all(value, axes, split_axis=0, concat_axis=0, tiled=True)  46.8 us
    pallas_call x11, Pallas kernels, call(): pl.pallas_call(functools.partial(body, length, rows), out_shape=outs, in_...  35.9 us
    all_to_all x4, starting transfers between devices, move(): return lax.all_to_all(value, axes, split_axis=0, concat_axis=0, tiled=True)  16.2 us
    unnamed x62, local copies, waits for them, and re-layouts  13.9 us
    pallas_call x2, Pallas kernels, reorder(): pl.pallas_call(functools.partial(body, length, rows), out_shape=jax.Shape...  5.79 us
  transfers between devices with their start and end apart: 4, of which 4 were waited for; matrix products, arithmetic and copies ran while one was open for 0% of the time, Pallas kernels for 5%

profile of v3, /device:TPU:0, one launch (start us, length us, event | category | flops | bytes accessed | tf_op | source)
XLA Modules:
  0.0 220.2 jit_solution(8035481217707644848)
XLA Ops:
  4.5 2.9 %shard_map.156 = (f32[32,32,128]{2,1,0:T(8,128)}, f32[8,128,256]{2,1,0:T(8,128)S(1)}) custom-call(f32[64,2048]{1,0:T(8,128)S(1)} %bitcast.6, f32[64,2048]{1,0:T(8,128)S(1)} %bitcast.7, f32[2,8,256]{2,1,0:T(8,128)S(1)} %copy-done.14, bf16[2,256,512]{2,1,0:T(8,128)(2,1)S(1)} %copy-done.8), custom_call_target="tpu_custom_call" | custom-call | flops 6000000000 | bytes 4194304 | tf_op jit(solution)/shard_map/pallas_call | solution.py:641
  8.3 7.3 %all-to-all-start = ((f32[32,32,128]{2,1,0:T(8,128)}), f32[32,32,128]{2,1,0:T(8,128)S(1)}, u32[]{:S(2)}, u32[]{:S(2)}) async-start(f32[32,32,128]{2,1,0:T(8,128)} %get-tuple-element.18), calls=%async_computation | async-start | bytes 1048576 | tf_op jit(solution)/shard_map/all_to_all | solution.py:652
  15.7 15.6 %all-to-all-done.source = f32[32,32,128]{2,1,0:T(8,128)S(1)} async-done(((f32[32,32,128]{2,1,0:T(8,128)}), f32[32,32,128]{2,1,0:T(8,128)S(1)}, u32[]{:S(2)}, u32[]{:S(2)}) %all-to-all-start) | async-done | bytes 524320 | tf_op jit(solution)/shard_map/all_to_all | solution.py:652
  31.3 2.9 %shard_map.157 = (f32[32,32,128]{2,1,0:T(8,128)}, f32[8,64,256]{2,1,0:T(8,128)S(1)}) custom-call(s32[1]{0:T(128)} %bitcast.device_ref, f32[32,32,128]{2,1,0:T(8,128)S(1)} %all-to-all-done.source, f32[2,8,256]{2,1,0:T(8,128)S(1)} %copy-done.17, bf16[2,512,512]{2,1,0:T(8,128)(2,1)S(1)} %copy-done.5, f32[2,8,256]{2,1,0:T(8,128)S(1)} %copy-done.16, ...), custom_call_target="tpu_custom_call" | custom-call | flops 6000000000 | bytes 4194304 | tf_op jit(solution)/shard_map/pallas_call | solution.py:641
  35.0 3.0 %all-to-all-start.1 = ((f32[32,32,128]{2,1,0:T(8,128)}), f32[32,32,128]{2,1,0:T(8,128)S(1)}, u32[]{:S(2)}, u32[]{:S(2)}) async-start(f32[32,32,128]{2,1,0:T(8,128)} %get-tuple-element.19), calls=%async_computation.1 | async-start | bytes 1048576 | tf_op jit(solution)/shard_map/all_to_all | solution.py:652
  40.3 2.7 %shard_map.158.second = f32[8,64,256]{2,1,0:T(8,128)S(1)} custom-call(f32[8,128,256]{2,1,0:T(8,128)S(1)} %copy-done.20, f32[2,8,256]{2,1,0:T(8,128)S(1)} %copy-done.15, bf16[2,256,512]{2,1,0:T(8,128)(2,1)S(1)} %copy-done.9, bf16[2,512,256]{2,1,0:T(8,128)(2,1)S(1)} %copy-done.7, s32[1,256]{1,0:T(1,128)S(1)} %copy-done.18), custom_call_target="tpu_custom_call" | custom-call | flops 6000000000 | bytes 4194304 | tf_op jit(solution)/shard_map/pallas_call | solution.py:641
  43.8 9.8 %all-to-all-done.1.source = f32[32,32,128]{2,1,0:T(8,128)S(1)} async-done(((f32[32,32,128]{2,1,0:T(8,128)}), f32[32,32,128]{2,1,0:T(8,128)S(1)}, u32[]{:S(2)}, u32[]{:S(2)}) %all-to-all-start.1) | async-done | bytes 524320 | tf_op jit(solution)/shard_map/all_to_all | solution.py:652
  55.7 4.2 %shard_map.159 = (f32[32,32,128]{2,1,0:T(8,128)}, f32[8,64,256]{2,1,0:T(8,128)S(1)}) custom-call(f32[32,32,128]{2,1,0:T(8,128)S(1)} %all-to-all-done.1.source, f32[8,64,256]{2,1,0:T(8,128)S(1)} %copy-done.25, f32[2,8,256]{2,1,0:T(8,128)S(1)} %copy-done.15, bf16[2,512,256]{2,1,0:T(8,128)(2,1)S(1)} %copy-done.7, bf16[2,256,512]{2,1,0:T(8,128)(2,1)S(1)} %copy-done.10), custom_call_target="tpu_custom_call" | custom-call | flops 6000000000 | bytes 4194304 | tf_op jit(solution)/shard_map/pallas_call | solution.py:641
  60.7 3.0 %all-to-all-start.2 = ((f32[32,32,128]{2,1,0:T(8,128)}), f32[32,32,128]{2,1,0:T(8,128)S(1)}, u32[]{:S(2)}, u32[]{:S(2)}) async-start(f32[32,32,128]{2,1,0:T(8,128)} %get-tuple-element.21), calls=%async_computation.2 | async-start | bytes 1048576 | tf_op jit(solution)/shard_map/all_to_all | solution.py:652
  63.7 2.9 %shard_map.160.forcing = f32[8,128,256]{2,1,0:T(8,128)} custom-call(f32[2,64,2048]{2,1,0:T(8,128)} %forcing.1), custom_call_target="tpu_custom_call" | custom-call | tf_op jit(solution)/shard_map/pallas_call | solution.py:686
  66.7 12.7 %all-to-all-done.2.source = f32[32,32,128]{2,1,0:T(8,128)S(1)} async-done(((f32[32,32,128]{2,1,0:T(8,128)}), f32[32,32,128]{2,1,0:T(8,128)S(1)}, u32[]{:S(2)}, u32[]{:S(2)}) %all-to-all-start.2) | async-done | bytes 524320 | tf_op jit(solution)/shard_map/all_to_all | solution.py:652
  81.6 3.4 %shard_map.161 = f32[32,64,128]{2,1,0:T(8,128)S(1)} custom-call(s32[1]{0:T(128)} %bitcast.device_ref, f32[32,32,128]{2,1,0:T(8,128)S(1)} %all-to-all-done.2.source, f32[8,64,256]{2,1,0:T(8,128)S(1)} %copy-done.23, f32[8,128,256]{2,1,0:T(8,128)S(1)} %copy-done.1, f32[2,8,256]{2,1,0:T(8,128)S(1)} %copy-done.17, bf16[2,512,512]{2,1,0:T(8,128)(2,1)S(1)} %copy-done.5, ...), custom_call_target="tpu_custom_call" | custom-call | flops 6000000000 | bytes 4194304 | tf_op jit(solution)/shard_map/pallas_call | solution.py:641
  85.0 28.7 %all_to_all.40.source = f32[32,64,128]{2,1,0:T(8,128)S(1)} all-to-all(f32[32,64,128]{2,1,0:T(8,128)S(1)} %shard_map.161), channel_id=1, replica_groups=mesh['px'=8,'py'=4] {'px','py'}, dimensions={0} | all-to-all | bytes 2097152 | tf_op jit(solution)/shard_map/all_to_all | solution.py:652
  113.8 4.7 %shard_map.162 = (f32[32,72,128]{2,1,0:T(8,128)S(1)}, f32[64,2048]{1,0:T(8,128)}) custom-call(f32[32,64,128]{2,1,0:T(8,128)S(1)} %all_to_all.40.source, f32[8,128,256]{2,1,0:T(8,128)S(1)} %copy-done.21, f32[2,8,256]{2,1,0:T(8,128)S(1)} %copy-done.16, bf16[2,512,512]{2,1,0:T(8,128)(2,1)S(1)} %copy-done.4, bf16[2,512,512]{2,1,0:T(8,128)(2,1)S(1)} %copy-done.6), custom_call_target="tpu_custom_call" | custom-call | flops 6000000000 | bytes 4194304 | tf_op jit(solution)/shard_map/pallas_call | solution.py:641
  118.5 34.0 %all_to_all.41.source = f32[32,72,128]{2,1,0:T(8,128)S(1)} all-to-all(f32[32,72,128]{2,1,0:T(8,128)S(1)} %get-tuple-element.24), channel_id=1, replica_groups=mesh['px'=8,'py'=4] {'px','py'}, dimensions={0} | all-to-all | bytes 2359296 | tf_op jit(solution)/shard_map/all_to_all | solution.py:652
  152.5 3.5 %shard_map.163 = (f32[32,32,128]{2,1,0:T(8,128)S(1)}, f32[8,128,256]{2,1,0:T(8,128)S(1)}, f32[8,64,256]{2,1,0:T(8,128)S(1)}, f32[8,128]{1,0:T(8,128)S(1)}) custom-call(s32[1]{0:T(128)} %bitcast.device_ref, f32[32,72,128]{2,1,0:T(8,128)S(1)} %all_to_all.41.source, f32[2,8,256]{2,1,0:T(8,128)S(1)} %copy-done.16, bf16[2,512,512]{2,1,0:T(8,128)(2,1)S(1)} %copy-done.6, ...), custom_call_target="tpu_custom_call" | custom-call | flops 6000000000 | bytes 4194304 | tf_op jit(solution)/shard_map/pallas_call | solution.py:641
  156.0 17.3 %all_to_all.42.source = f32[32,32,128]{2,1,0:T(8,128)S(1)} all-to-all(f32[32,32,128]{2,1,0:T(8,128)S(1)} %get-tuple-element.26), channel_id=1, replica_groups=mesh['px'=8,'py'=4] {'px','py'}, dimensions={0} | all-to-all | bytes 1048576 | tf_op jit(solution)/shard_map/all_to_all | solution.py:652
  173.3 3.4 %shard_map.164 = (f32[32,32,128]{2,1,0:T(8,128)S(1)}, f32[8,64,256]{2,1,0:T(8,128)S(1)}) custom-call(f32[32,32,128]{2,1,0:T(8,128)S(1)} %all_to_all.42.source, f32[8,64,256]{2,1,0:T(8,128)S(1)} %copy-done.28, f32[8,64,256]{2,1,0:T(8,128)S(1)} %copy-done.26, f32[2,8,256]{2,1,0:T(8,128)S(1)} %copy-done.15, bf16[2,512,256]{2,1,0:T(8,128)(2,1)S(1)} %copy-done.7, ...), custom_call_target="tpu_custom_call" | custom-call | flops 6000000000 | bytes 4194304 | tf_op jit(solution)/shard_map/pallas_call | solution.py:641
  176.8 18.3 %all_to_all.43.source = f32[32,32,128]{2,1,0:T(8,128)S(1)} all-to-all(f32[32,32,128]{2,1,0:T(8,128)S(1)} %get-tuple-element.28), channel_id=1, replica_groups=mesh['px'=8,'py'=4] {'px','py'}, dimensions={0} | all-to-all | bytes 1048576 | tf_op jit(solution)/shard_map/all_to_all | solution.py:652
  195.1 2.9 %shard_map.165 = f32[32,32,128]{2,1,0:T(8,128)} custom-call(s32[1]{0:T(128)} %bitcast.device_ref, f32[32,32,128]{2,1,0:T(8,128)S(1)} %all_to_all.43.source, f32[8,64,256]{2,1,0:T(8,128)S(1)} %get-tuple-element.29.coef, f32[2,8,256]{2,1,0:T(8,128)S(1)} %copy-done.17, bf16[2,512,512]{2,1,0:T(8,128)(2,1)S(1)} %copy-done.5, f32[2,8,256]{2,1,0:T(8,128)S(1)} %copy-done.16, ...), custom_call_target="tpu_custom_call" | custom-call | flops 6000000000 | bytes 4194304 | tf_op jit(solution)/shard_map/pallas_call | solution.py:641
  198.0 3.0 %all-to-all-start.7 = ((f32[32,32,128]{2,1,0:T(8,128)}), f32[32,32,128]{2,1,0:T(8,128)S(1)}, u32[]{:S(2)}, u32[]{:S(2)}) async-start(f32[32,32,128]{2,1,0:T(8,128)} %shard_map.165), calls=%async_computation.7 | async-start | bytes 1048576 | tf_op jit(solution)/shard_map/all_to_all | solution.py:652
  201.5 2.9 %shard_map.168 = f32[2,64,2048]{2,1,0:T(8,128)} custom-call(f32[8,128,256]{2,1,0:T(8,128)} %copy-done), custom_call_target="tpu_custom_call" | custom-call | tf_op jit(solution)/shard_map/pallas_call | solution.py:686
  205.0 2.8 %shard_map.166.second = f32[8,64,256]{2,1,0:T(8,128)S(1)} custom-call(f32[8,64,256]{2,1,0:T(8,128)S(1)} %copy-done.30, f32[2,8,256]{2,1,0:T(8,128)S(1)} %copy-done.15, bf16[2,256,512]{2,1,0:T(8,128)(2,1)S(1)} %copy-done.12, bf16[2,512,256]{2,1,0:T(8,128)(2,1)S(1)} %copy-done.7, s32[1,256]{1,0:T(1,128)S(1)} %copy-done.18), custom_call_target="tpu_custom_call" | custom-call | flops 6000000000 | bytes 4194304 | tf_op jit(solution)/shard_map/pallas_call | solution.py:641
  207.8 8.8 %all-to-all-done.7.source = f32[32,32,128]{2,1,0:T(8,128)S(1)} async-done(((f32[32,32,128]{2,1,0:T(8,128)}), f32[32,32,128]{2,1,0:T(8,128)S(1)}, u32[]{:S(2)}, u32[]{:S(2)}) %all-to-all-start.7) | async-done | bytes 524320 | tf_op jit(solution)/shard_map/all_to_all | solution.py:652
  (64 shorter events, 16.9 us)
Async XLA Ops:
  4.5 26.8 %copy-start.4 = (bf16[2,512,512]{2,1,0:T(8,128)(2,1)S(1)}, bf16[2,512,512]{2,1,0:T(8,128)(2,1)}, u32[]{:S(2)}) copy-start(bf16[2,512,512]{2,1,0:T(8,128)(2,1)} %constant.43.clone.out_matrix.in_matrix) | copy-start | bytes 3145732
  4.5 26.8 %copy-start.5 = (bf16[2,512,512]{2,1,0:T(8,128)(2,1)S(1)}, bf16[2,512,512]{2,1,0:T(8,128)(2,1)}, u32[]{:S(2)}) copy-start(bf16[2,512,512]{2,1,0:T(8,128)(2,1)} %constant.42.clone.in_matrix) | copy-start | bytes 3145732
  4.5 26.8 %copy-start.16 = (f32[2,8,256]{2,1,0:T(8,128)S(1)}, f32[2,8,256]{2,1,0:T(8,128)}, u32[]{:S(2)}) copy-start(f32[2,8,256]{2,1,0:T(8,128)} %constant.35.clone.out_twiddle.twiddle.in_twiddle) | copy-start | bytes 49156
  4.5 26.8 %copy-start.17 = (f32[2,8,256]{2,1,0:T(8,128)S(1)}, f32[2,8,256]{2,1,0:T(8,128)}, u32[]{:S(2)}) copy-start(f32[2,8,256]{2,1,0:T(8,128)} %constant.37.clone.in_twiddle) | copy-start | bytes 49156
  8.3 22.9 %all-to-all-start = ((f32[32,32,128]{2,1,0:T(8,128)}), f32[32,32,128]{2,1,0:T(8,128)S(1)}, u32[]{:S(2)}, u32[]{:S(2)}) async-start(f32[32,32,128]{2,1,0:T(8,128)} %get-tuple-element.18), calls=%async_computation | async-start | bytes 1048576 | tf_op jit(solution)/shard_map/all_to_all | solution.py:652
  31.3 6.7 %copy-start.7 = (bf16[2,512,256]{2,1,0:T(8,128)(2,1)S(1)}, bf16[2,512,256]{2,1,0:T(8,128)(2,1)}, u32[]{:S(2)}) copy-start(bf16[2,512,256]{2,1,0:T(8,128)(2,1)} %constant.41.clone.in_matrix) | copy-start | bytes 1572868
  31.3 6.7 %copy-start.15 = (f32[2,8,256]{2,1,0:T(8,128)S(1)}, f32[2,8,256]{2,1,0:T(8,128)}, u32[]{:S(2)}) copy-start(f32[2,8,256]{2,1,0:T(8,128)} %constant.36.clone.twiddle) | copy-start | bytes 49156
  31.3 6.7 %copy-start.18 = (s32[1,256]{1,0:T(1,128)S(1)}, s32[1,256]{1,0:T(1,128)}, u32[]{:S(2)}) copy-start(s32[1,256]{1,0:T(1,128)} %constant.39.clone.kept) | copy-start | bytes 3076
  35.0 18.6 %all-to-all-start.1 = ((f32[32,32,128]{2,1,0:T(8,128)}), f32[32,32,128]{2,1,0:T(8,128)S(1)}, u32[]{:S(2)}, u32[]{:S(2)}) async-start(f32[32,32,128]{2,1,0:T(8,128)} %get-tuple-element.19), calls=%async_computation.1 | async-start | bytes 1048576 | tf_op jit(solution)/shard_map/all_to_all | solution.py:652
  38.0 1.0 copy-start.9
  39.0 1.2 copy-start.20
  60.7 18.6 %all-to-all-start.2 = ((f32[32,32,128]{2,1,0:T(8,128)}), f32[32,32,128]{2,1,0:T(8,128)S(1)}, u32[]{:S(2)}, u32[]{:S(2)}) async-start(f32[32,32,128]{2,1,0:T(8,128)} %get-tuple-element.21), calls=%async_computation.2 | async-start | bytes 1048576 | tf_op jit(solution)/shard_map/all_to_all | solution.py:652
  63.7 15.6 %copy-start.13 = (bf16[2,256,256]{2,1,0:T(8,128)(2,1)S(1)}, bf16[2,256,256]{2,1,0:T(8,128)(2,1)}, u32[]{:S(2)}) copy-start(bf16[2,256,256]{2,1,0:T(8,128)(2,1)} %constant.38.clone.mirror) | copy-start | bytes 786436
  79.3 1.2 copy-start.1
  85.0 28.7 %copy-start.6 = (bf16[2,512,512]{2,1,0:T(8,128)(2,1)S(1)}, bf16[2,512,512]{2,1,0:T(8,128)(2,1)}, u32[]{:S(2)}) copy-start(bf16[2,512,512]{2,1,0:T(8,128)(2,1)} %constant.44.clone.out_matrix.in_matrix) | copy-start | bytes 3145732
  85.0 28.7 %copy-start.21 = (f32[8,128,256]{2,1,0:T(8,128)S(1)}, f32[8,128,256]{2,1,0:T(8,128)}, u32[]{:S(2)}) copy-start(f32[8,128,256]{2,1,0:T(8,128)} %copy-done.19) | copy-start | bytes 3145732
  152.5 20.8 %copy-start.11 = (bf16[2,256,512]{2,1,0:T(8,128)(2,1)S(1)}, bf16[2,256,512]{2,1,0:T(8,128)(2,1)}, u32[]{:S(2)}) copy-start(bf16[2,256,512]{2,1,0:T(8,128)(2,1)} %constant.40.clone.matrix.out_matrix) | copy-start | bytes 1572868
  152.5 20.8 %copy-start.26 = (f32[8,64,256]{2,1,0:T(8,128)S(1)}, f32[8,64,256]{2,1,0:T(8,128)}, u32[]{:S(2)}) copy-start(f32[8,64,256]{2,1,0:T(8,128)} %copy-done.24) | copy-start | bytes 1572868
  152.5 20.8 %copy-start.28 = (f32[8,64,256]{2,1,0:T(8,128)S(1)}, f32[8,64,256]{2,1,0:T(8,128)}, u32[]{:S(2)}) copy-start(f32[8,64,256]{2,1,0:T(8,128)} %copy-done.27) | copy-start | bytes 1572868
  156.0 20.8 %copy-start = (f32[8,128,256]{2,1,0:T(8,128)}, f32[8,128,256]{2,1,0:T(8,128)S(1)}, u32[]{:S(2)}) copy-start(f32[8,128,256]{2,1,0:T(8,128)S(1)} %get-tuple-element.31.slabs) | copy-start | bytes 3145732
  176.8 18.3 %copy-start.29 = (f32[8,64,256]{2,1,0:T(8,128)}, f32[8,64,256]{2,1,0:T(8,128)S(1)}, u32[]{:S(2)}) copy-start(f32[8,64,256]{2,1,0:T(8,128)S(1)} %get-tuple-element.30.field_p) | copy-start | bytes 1572868
  198.0 18.6 %all-to-all-start.7 = ((f32[32,32,128]{2,1,0:T(8,128)}), f32[32,32,128]{2,1,0:T(8,128)S(1)}, u32[]{:S(2)}, u32[]{:S(2)}) async-start(f32[32,32,128]{2,1,0:T(8,128)} %shard_map.165), calls=%async_computation.7 | async-start | bytes 1048576 | tf_op jit(solution)/shard_map/all_to_all | solution.py:652
  201.0 4.0 %copy-start.12 = (bf16[2,256,512]{2,1,0:T(8,128)(2,1)S(1)}, bf16[2,256,512]{2,1,0:T(8,128)(2,1)}, u32[]{:S(2)}) copy-start(bf16[2,256,512]{2,1,0:T(8,128)(2,1)} %constant.40.clone.matrix.out_matrix) | copy-start | bytes 1572868
  201.0 4.0 %copy-start.30 = (f32[8,64,256]{2,1,0:T(8,128)S(1)}, f32[8,64,256]{2,1,0:T(8,128)}, u32[]{:S(2)}) copy-start(f32[8,64,256]{2,1,0:T(8,128)} %copy-done.29) | copy-start | bytes 1572868
  (11 other events, 10.4 us)

commit v4 on v3

--- a/solution.py
+++ b/solution.py
@@ -644,7 +644,7 @@
             in_specs=[smem if operand is device else vmem for operand in operands],
             out_specs=jax.tree.map(lambda leaf: vmem, outs),
             scratch_shapes=scratch,
-            compiler_params=pltpu.CompilerParams(vmem_limit_bytes=20 * 2**20),
+            compiler_params=pltpu.CompilerParams(vmem_limit_bytes=12 * 2**20),
             cost_estimate=pl.CostEstimate(flops=6 * 10**9, bytes_accessed=4 * 2**20, transcendentals=0),
         )(*operands)
 

time: 221 us -> 221 us (level)
  no operation moved by 1% of the time
where the time goes in v4:
time: 221 us; the launch traced here: 220 us
  blocking collectives  98.4 us (45%)
  waiting for transfers between devices  46.8 us (21%)
  Pallas kernels  41.7 us (19%)
  starting transfers between devices  16.2 us (7%)
  local copies, waits for them, and re-layouts  14.4 us (7%)
  between operations  2.67 us (1%)
    all_to_all x4, blocking collectives, move(): return lax.all_to_all(value, axes, split_axis=0, concat_axis=0, tiled=True)  98.4 us
    all_to_all x4, waiting for transfers between devices, move(): return lax.all_to_all(value, axes, split_axis=0, concat_axis=0, tiled=True)  46.8 us
    pallas_call x11, Pallas kernels, call(): pl.pallas_call(functools.partial(body, length, rows), out_shape=outs, in_...  35.9 us
    all_to_all x4, starting transfers between devices, move(): return lax.all_to_all(value, axes, split_axis=0, concat_axis=0, tiled=True)  16.2 us
    unnamed x62, local copies, waits for them, and re-layouts  13.9 us
    pallas_call x2, Pallas kernels, reorder(): pl.pallas_call(functools.partial(body, length, rows), out_shape=jax.Shape...  5.79 us
  transfers between devices with their start and end apart: 4, of which 4 were waited for; matrix products, arithmetic and copies ran while one was open for 0% of the time, Pallas kernels for 5%

profile of v4, /device:TPU:0, one launch (start us, length us, event | category | flops | bytes accessed | tf_op | source)
XLA Modules:
  0.0 220.2 jit_solution(7768365268751592473)
XLA Ops:
  4.5 2.9 %shard_map.156 = (f32[32,32,128]{2,1,0:T(8,128)}, f32[8,128,256]{2,1,0:T(8,128)S(1)}) custom-call(f32[64,2048]{1,0:T(8,128)S(1)} %bitcast.6, f32[64,2048]{1,0:T(8,128)S(1)} %bitcast.7, f32[2,8,256]{2,1,0:T(8,128)S(1)} %copy-done.14, bf16[2,256,512]{2,1,0:T(8,128)(2,1)S(1)} %copy-done.8), custom_call_target="tpu_custom_call" | custom-call | flops 6000000000 | bytes 4194304 | tf_op jit(solution)/shard_map/pallas_call | solution.py:641
  8.3 7.3 %all-to-all-start = ((f32[32,32,128]{2,1,0:T(8,128)}), f32[32,32,128]{2,1,0:T(8,128)S(1)}, u32[]{:S(2)}, u32[]{:S(2)}) async-start(f32[32,32,128]{2,1,0:T(8,128)} %get-tuple-element.18), calls=%async_computation | async-start | bytes 1048576 | tf_op jit(solution)/shard_map/all_to_all | solution.py:652
  15.7 15.6 %all-to-all-done.source = f32[32,32,128]{2,1,0:T(8,128)S(1)} async-done(((f32[32,32,128]{2,1,0:T(8,128)}), f32[32,32,128]{2,1,0:T(8,128)S(1)}, u32[]{:S(2)}, u32[]{:S(2)}) %all-to-all-start) | async-done | bytes 524320 | tf_op jit(solution)/shard_map/all_to_all | solution.py:652
  31.3 2.9 %shard_map.157 = (f32[32,32,128]{2,1,0:T(8,128)}, f32[8,64,256]{2,1,0:T(8,128)S(1)}) custom-call(s32[1]{0:T(128)} %bitcast.device_ref, f32[32,32,128]{2,1,0:T(8,128)S(1)} %all-to-all-done.source, f32[2,8,256]{2,1,0:T(8,128)S(1)} %copy-done.17, bf16[2,512,512]{2,1,0:T(8,128)(2,1)S(1)} %copy-done.5, f32[2,8,256]{2,1,0:T(8,128)S(1)} %copy-done.16, ...), custom_call_target="tpu_custom_call" | custom-call | flops 6000000000 | bytes 4194304 | tf_op jit(solution)/shard_map/pallas_call | solution.py:641
  35.0 3.0 %all-to-all-start.1 = ((f32[32,32,128]{2,1,0:T(8,128)}), f32[32,32,128]{2,1,0:T(8,128)S(1)}, u32[]{:S(2)}, u32[]{:S(2)}) async-start(f32[32,32,128]{2,1,0:T(8,128)} %get-tuple-element.19), calls=%async_computation.1 | async-start | bytes 1048576 | tf_op jit(solution)/shard_map/all_to_all | solution.py:652
  40.3 2.7 %shard_map.158.second = f32[8,64,256]{2,1,0:T(8,128)S(1)} custom-call(f32[8,128,256]{2,1,0:T(8,128)S(1)} %copy-done.20, f32[2,8,256]{2,1,0:T(8,128)S(1)} %copy-done.15, bf16[2,256,512]{2,1,0:T(8,128)(2,1)S(1)} %copy-done.9, bf16[2,512,256]{2,1,0:T(8,128)(2,1)S(1)} %copy-done.7, s32[1,256]{1,0:T(1,128)S(1)} %copy-done.18), custom_call_target="tpu_custom_call" | custom-call | flops 6000000000 | bytes 4194304 | tf_op jit(solution)/shard_map/pallas_call | solution.py:641
  43.8 9.8 %all-to-all-done.1.source = f32[32,32,128]{2,1,0:T(8,128)S(1)} async-done(((f32[32,32,128]{2,1,0:T(8,128)}), f32[32,32,128]{2,1,0:T(8,128)S(1)}, u32[]{:S(2)}, u32[]{:S(2)}) %all-to-all-start.1) | async-done | bytes 524320 | tf_op jit(solution)/shard_map/all_to_all | solution.py:652
  55.7 4.2 %shard_map.159 = (f32[32,32,128]{2,1,0:T(8,128)}, f32[8,64,256]{2,1,0:T(8,128)S(1)}) custom-call(f32[32,32,128]{2,1,0:T(8,128)S(1)} %all-to-all-done.1.source, f32[8,64,256]{2,1,0:T(8,128)S(1)} %copy-done.25, f32[2,8,256]{2,1,0:T(8,128)S(1)} %copy-done.15, bf16[2,512,256]{2,1,0:T(8,128)(2,1)S(1)} %copy-done.7, bf16[2,256,512]{2,1,0:T(8,128)(2,1)S(1)} %copy-done.10), custom_call_target="tpu_custom_call" | custom-call | flops 6000000000 | bytes 4194304 | tf_op jit(solution)/shard_map/pallas_call | solution.py:641
  60.7 3.0 %all-to-all-start.2 = ((f32[32,32,128]{2,1,0:T(8,128)}), f32[32,32,128]{2,1,0:T(8,128)S(1)}, u32[]{:S(2)}, u32[]{:S(2)}) async-start(f32[32,32,128]{2,1,0:T(8,128)} %get-tuple-element.21), calls=%async_computation.2 | async-start | bytes 1048576 | tf_op jit(solution)/shard_map/all_to_all | solution.py:652
  63.7 2.9 %shard_map.160.forcing = f32[8,128,256]{2,1,0:T(8,128)} custom-call(f32[2,64,2048]{2,1,0:T(8,128)} %forcing.1), custom_call_target="tpu_custom_call" | custom-call | tf_op jit(solution)/shard_map/pallas_call | solution.py:686
  66.7 12.7 %all-to-all-done.2.source = f32[32,32,128]{2,1,0:T(8,128)S(1)} async-done(((f32[32,32,128]{2,1,0:T(8,128)}), f32[32,32,128]{2,1,0:T(8,128)S(1)}, u32[]{:S(2)}, u32[]{:S(2)}) %all-to-all-start.2) | async-done | bytes 524320 | tf_op jit(solution)/shard_map/all_to_all | solution.py:652
  81.6 3.4 %shard_map.161 = f32[32,64,128]{2,1,0:T(8,128)S(1)} custom-call(s32[1]{0:T(128)} %bitcast.device_ref, f32[32,32,128]{2,1,0:T(8,128)S(1)} %all-to-all-done.2.source, f32[8,64,256]{2,1,0:T(8,128)S(1)} %copy-done.23, f32[8,128,256]{2,1,0:T(8,128)S(1)} %copy-done.1, f32[2,8,256]{2,1,0:T(8,128)S(1)} %copy-done.17, bf16[2,512,512]{2,1,0:T(8,128)(2,1)S(1)} %copy-done.5, ...), custom_call_target="tpu_custom_call" | custom-call | flops 6000000000 | bytes 4194304 | tf_op jit(solution)/shard_map/pallas_call | solution.py:641
  85.0 28.7 %all_to_all.40.source = f32[32,64,128]{2,1,0:T(8,128)S(1)} all-to-all(f32[32,64,128]{2,1,0:T(8,128)S(1)} %shard_map.161), channel_id=1, replica_groups=mesh['px'=8,'py'=4] {'px','py'}, dimensions={0} | all-to-all | bytes 2097152 | tf_op jit(solution)/shard_map/all_to_all | solution.py:652
  113.8 4.7 %shard_map.162 = (f32[32,72,128]{2,1,0:T(8,128)S(1)}, f32[64,2048]{1,0:T(8,128)}) custom-call(f32[32,64,128]{2,1,0:T(8,128)S(1)} %all_to_all.40.source, f32[8,128,256]{2,1,0:T(8,128)S(1)} %copy-done.21, f32[2,8,256]{2,1,0:T(8,128)S(1)} %copy-done.16, bf16[2,512,512]{2,1,0:T(8,128)(2,1)S(1)} %copy-done.4, bf16[2,512,512]{2,1,0:T(8,128)(2,1)S(1)} %copy-done.6), custom_call_target="tpu_custom_call" | custom-call | flops 6000000000 | bytes 4194304 | tf_op jit(solution)/shard_map/pallas_call | solution.py:641
  118.5 34.0 %all_to_all.41.source = f32[32,72,128]{2,1,0:T(8,128)S(1)} all-to-all(f32[32,72,128]{2,1,0:T(8,128)S(1)} %get-tuple-element.24), channel_id=1, replica_groups=mesh['px'=8,'py'=4] {'px','py'}, dimensions={0} | all-to-all | bytes 2359296 | tf_op jit(solution)/shard_map/all_to_all | solution.py:652
  152.5 3.5 %shard_map.163 = (f32[32,32,128]{2,1,0:T(8,128)S(1)}, f32[8,128,256]{2,1,0:T(8,128)S(1)}, f32[8,64,256]{2,1,0:T(8,128)S(1)}, f32[8,128]{1,0:T(8,128)S(1)}) custom-call(s32[1]{0:T(128)} %bitcast.device_ref, f32[32,72,128]{2,1,0:T(8,128)S(1)} %all_to_all.41.source, f32[2,8,256]{2,1,0:T(8,128)S(1)} %copy-done.16, bf16[2,512,512]{2,1,0:T(8,128)(2,1)S(1)} %copy-done.6, ...), custom_call_target="tpu_custom_call" | custom-call | flops 6000000000 | bytes 4194304 | tf_op jit(solution)/shard_map/pallas_call | solution.py:641
  156.0 17.3 %all_to_all.42.source = f32[32,32,128]{2,1,0:T(8,128)S(1)} all-to-all(f32[32,32,128]{2,1,0:T(8,128)S(1)} %get-tuple-element.26), channel_id=1, replica_groups=mesh['px'=8,'py'=4] {'px','py'}, dimensions={0} | all-to-all | bytes 1048576 | tf_op jit(solution)/shard_map/all_to_all | solution.py:652
  173.3 3.4 %shard_map.164 = (f32[32,32,128]{2,1,0:T(8,128)S(1)}, f32[8,64,256]{2,1,0:T(8,128)S(1)}) custom-call(f32[32,32,128]{2,1,0:T(8,128)S(1)} %all_to_all.42.source, f32[8,64,256]{2,1,0:T(8,128)S(1)} %copy-done.28, f32[8,64,256]{2,1,0:T(8,128)S(1)} %copy-done.26, f32[2,8,256]{2,1,0:T(8,128)S(1)} %copy-done.15, bf16[2,512,256]{2,1,0:T(8,128)(2,1)S(1)} %copy-done.7, ...), custom_call_target="tpu_custom_call" | custom-call | flops 6000000000 | bytes 4194304 | tf_op jit(solution)/shard_map/pallas_call | solution.py:641
  176.8 18.3 %all_to_all.43.source = f32[32,32,128]{2,1,0:T(8,128)S(1)} all-to-all(f32[32,32,128]{2,1,0:T(8,128)S(1)} %get-tuple-element.28), channel_id=1, replica_groups=mesh['px'=8,'py'=4] {'px','py'}, dimensions={0} | all-to-all | bytes 1048576 | tf_op jit(solution)/shard_map/all_to_all | solution.py:652
  195.1 2.9 %shard_map.165 = f32[32,32,128]{2,1,0:T(8,128)} custom-call(s32[1]{0:T(128)} %bitcast.device_ref, f32[32,32,128]{2,1,0:T(8,128)S(1)} %all_to_all.43.source, f32[8,64,256]{2,1,0:T(8,128)S(1)} %get-tuple-element.29.coef, f32[2,8,256]{2,1,0:T(8,128)S(1)} %copy-done.17, bf16[2,512,512]{2,1,0:T(8,128)(2,1)S(1)} %copy-done.5, f32[2,8,256]{2,1,0:T(8,128)S(1)} %copy-done.16, ...), custom_call_target="tpu_custom_call" | custom-call | flops 6000000000 | bytes 4194304 | tf_op jit(solution)/shard_map/pallas_call | solution.py:641
  198.0 3.0 %all-to-all-start.7 = ((f32[32,32,128]{2,1,0:T(8,128)}), f32[32,32,128]{2,1,0:T(8,128)S(1)}, u32[]{:S(2)}, u32[]{:S(2)}) async-start(f32[32,32,128]{2,1,0:T(8,128)} %shard_map.165), calls=%async_computation.7 | async-start | bytes 1048576 | tf_op jit(solution)/shard_map/all_to_all | solution.py:652
  201.5 2.9 %shard_map.168 = f32[2,64,2048]{2,1,0:T(8,128)} custom-call(f32[8,128,256]{2,1,0:T(8,128)} %copy-done), custom_call_target="tpu_custom_call" | custom-call | tf_op jit(solution)/shard_map/pallas_call | solution.py:686
  205.0 2.8 %shard_map.166.second = f32[8,64,256]{2,1,0:T(8,128)S(1)} custom-call(f32[8,64,256]{2,1,0:T(8,128)S(1)} %copy-done.30, f32[2,8,256]{2,1,0:T(8,128)S(1)} %copy-done.15, bf16[2,256,512]{2,1,0:T(8,128)(2,1)S(1)} %copy-done.12, bf16[2,512,256]{2,1,0:T(8,128)(2,1)S(1)} %copy-done.7, s32[1,256]{1,0:T(1,128)S(1)} %copy-done.18), custom_call_target="tpu_custom_call" | custom-call | flops 6000000000 | bytes 4194304 | tf_op jit(solution)/shard_map/pallas_call | solution.py:641
  207.8 8.8 %all-to-all-done.7.source = f32[32,32,128]{2,1,0:T(8,128)S(1)} async-done(((f32[32,32,128]{2,1,0:T(8,128)}), f32[32,32,128]{2,1,0:T(8,128)S(1)}, u32[]{:S(2)}, u32[]{:S(2)}) %all-to-all-start.7) | async-done | bytes 524320 | tf_op jit(solution)/shard_map/all_to_all | solution.py:652
  (64 shorter events, 16.9 us)
Async XLA Ops:
  4.5 26.8 %copy-start.4 = (bf16[2,512,512]{2,1,0:T(8,128)(2,1)S(1)}, bf16[2,512,512]{2,1,0:T(8,128)(2,1)}, u32[]{:S(2)}) copy-start(bf16[2,512,512]{2,1,0:T(8,128)(2,1)} %constant.43.clone.out_matrix.in_matrix) | copy-start | bytes 3145732
  4.5 26.8 %copy-start.5 = (bf16[2,512,512]{2,1,0:T(8,128)(2,1)S(1)}, bf16[2,512,512]{2,1,0:T(8,128)(2,1)}, u32[]{:S(2)}) copy-start(bf16[2,512,512]{2,1,0:T(8,128)(2,1)} %constant.42.clone.in_matrix) | copy-start | bytes 3145732
  4.5 26.8 %copy-start.16 = (f32[2,8,256]{2,1,0:T(8,128)S(1)}, f32[2,8,256]{2,1,0:T(8,128)}, u32[]{:S(2)}) copy-start(f32[2,8,256]{2,1,0:T(8,128)} %constant.35.clone.out_twiddle.twiddle.in_twiddle) | copy-start | bytes 49156
  4.5 26.8 %copy-start.17 = (f32[2,8,256]{2,1,0:T(8,128)S(1)}, f32[2,8,256]{2,1,0:T(8,128)}, u32[]{:S(2)}) copy-start(f32[2,8,256]{2,1,0:T(8,128)} %constant.37.clone.in_twiddle) | copy-start | bytes 49156
  8.3 22.9 %all-to-all-start = ((f32[32,32,128]{2,1,0:T(8,128)}), f32[32,32,128]{2,1,0:T(8,128)S(1)}, u32[]{:S(2)}, u32[]{:S(2)}) async-start(f32[32,32,128]{2,1,0:T(8,128)} %get-tuple-element.18), calls=%async_computation | async-start | bytes 1048576 | tf_op jit(solution)/shard_map/all_to_all | solution.py:652
  31.3 6.7 %copy-start.7 = (bf16[2,512,256]{2,1,0:T(8,128)(2,1)S(1)}, bf16[2,512,256]{2,1,0:T(8,128)(2,1)}, u32[]{:S(2)}) copy-start(bf16[2,512,256]{2,1,0:T(8,128)(2,1)} %constant.41.clone.in_matrix) | copy-start | bytes 1572868
  31.3 6.7 %copy-start.15 = (f32[2,8,256]{2,1,0:T(8,128)S(1)}, f32[2,8,256]{2,1,0:T(8,128)}, u32[]{:S(2)}) copy-start(f32[2,8,256]{2,1,0:T(8,128)} %constant.36.clone.twiddle) | copy-start | bytes 49156
  31.3 6.7 %copy-start.18 = (s32[1,256]{1,0:T(1,128)S(1)}, s32[1,256]{1,0:T(1,128)}, u32[]{:S(2)}) copy-start(s32[1,256]{1,0:T(1,128)} %constant.39.clone.kept) | copy-start | bytes 3076
  35.0 18.6 %all-to-all-start.1 = ((f32[32,32,128]{2,1,0:T(8,128)}), f32[32,32,128]{2,1,0:T(8,128)S(1)}, u32[]{:S(2)}, u32[]{:S(2)}) async-start(f32[32,32,128]{2,1,0:T(8,128)} %get-tuple-element.19), calls=%async_computation.1 | async-start | bytes 1048576 | tf_op jit(solution)/shard_map/all_to_all | solution.py:652
  38.0 1.0 copy-start.9
  39.0 1.2 copy-start.20
  60.7 18.6 %all-to-all-start.2 = ((f32[32,32,128]{2,1,0:T(8,128)}), f32[32,32,128]{2,1,0:T(8,128)S(1)}, u32[]{:S(2)}, u32[]{:S(2)}) async-start(f32[32,32,128]{2,1,0:T(8,128)} %get-tuple-element.21), calls=%async_computation.2 | async-start | bytes 1048576 | tf_op jit(solution)/shard_map/all_to_all | solution.py:652
  63.7 15.6 %copy-start.13 = (bf16[2,256,256]{2,1,0:T(8,128)(2,1)S(1)}, bf16[2,256,256]{2,1,0:T(8,128)(2,1)}, u32[]{:S(2)}) copy-start(bf16[2,256,256]{2,1,0:T(8,128)(2,1)} %constant.38.clone.mirror) | copy-start | bytes 786436
  79.3 1.2 copy-start.1
  85.0 28.7 %copy-start.6 = (bf16[2,512,512]{2,1,0:T(8,128)(2,1)S(1)}, bf16[2,512,512]{2,1,0:T(8,128)(2,1)}, u32[]{:S(2)}) copy-start(bf16[2,512,512]{2,1,0:T(8,128)(2,1)} %constant.44.clone.out_matrix.in_matrix) | copy-start | bytes 3145732
  85.0 28.7 %copy-start.21 = (f32[8,128,256]{2,1,0:T(8,128)S(1)}, f32[8,128,256]{2,1,0:T(8,128)}, u32[]{:S(2)}) copy-start(f32[8,128,256]{2,1,0:T(8,128)} %copy-done.19) | copy-start | bytes 3145732
  152.5 20.8 %copy-start.11 = (bf16[2,256,512]{2,1,0:T(8,128)(2,1)S(1)}, bf16[2,256,512]{2,1,0:T(8,128)(2,1)}, u32[]{:S(2)}) copy-start(bf16[2,256,512]{2,1,0:T(8,128)(2,1)} %constant.40.clone.matrix.out_matrix) | copy-start | bytes 1572868
  152.5 20.8 %copy-start.26 = (f32[8,64,256]{2,1,0:T(8,128)S(1)}, f32[8,64,256]{2,1,0:T(8,128)}, u32[]{:S(2)}) copy-start(f32[8,64,256]{2,1,0:T(8,128)} %copy-done.24) | copy-start | bytes 1572868
  152.5 20.8 %copy-start.28 = (f32[8,64,256]{2,1,0:T(8,128)S(1)}, f32[8,64,256]{2,1,0:T(8,128)}, u32[]{:S(2)}) copy-start(f32[8,64,256]{2,1,0:T(8,128)} %copy-done.27) | copy-start | bytes 1572868
  156.0 20.8 %copy-start = (f32[8,128,256]{2,1,0:T(8,128)}, f32[8,128,256]{2,1,0:T(8,128)S(1)}, u32[]{:S(2)}) copy-start(f32[8,128,256]{2,1,0:T(8,128)S(1)} %get-tuple-element.31.slabs) | copy-start | bytes 3145732
  176.8 18.3 %copy-start.29 = (f32[8,64,256]{2,1,0:T(8,128)}, f32[8,64,256]{2,1,0:T(8,128)S(1)}, u32[]{:S(2)}) copy-start(f32[8,64,256]{2,1,0:T(8,128)S(1)} %get-tuple-element.30.field_p) | copy-start | bytes 1572868
  198.0 18.6 %all-to-all-start.7 = ((f32[32,32,128]{2,1,0:T(8,128)}), f32[32,32,128]{2,1,0:T(8,128)S(1)}, u32[]{:S(2)}, u32[]{:S(2)}) async-start(f32[32,32,128]{2,1,0:T(8,128)} %shard_map.165), calls=%async_computation.7 | async-start | bytes 1048576 | tf_op jit(solution)/shard_map/all_to_all | solution.py:652
  201.0 4.0 %copy-start.12 = (bf16[2,256,512]{2,1,0:T(8,128)(2,1)S(1)}, bf16[2,256,512]{2,1,0:T(8,128)(2,1)}, u32[]{:S(2)}) copy-start(bf16[2,256,512]{2,1,0:T(8,128)(2,1)} %constant.40.clone.matrix.out_matrix) | copy-start | bytes 1572868
  201.0 4.0 %copy-start.30 = (f32[8,64,256]{2,1,0:T(8,128)S(1)}, f32[8,64,256]{2,1,0:T(8,128)}, u32[]{:S(2)}) copy-start(f32[8,64,256]{2,1,0:T(8,128)} %copy-done.29) | copy-start | bytes 1572868
  (11 other events, 10.4 us)
